TPU v7x, 16 devices: a whole 2x2x2 slice. The times are simulated.
16 devices in a mesh: fs: 2 (over z), pp: 2 (over y), ep: 4 (over x, core).
Axes of the slice: x: 2, y: 2, z: 2, core: 2. Of those that a mesh axis runs over, the one named last changes fastest.
Arguments:
- w_gate: bfloat16 [2, 32, 2048, 768], P('pp', 'ep', None, 'fs')
- w_up: bfloat16 [2, 32, 2048, 768], P('pp', 'ep', None, 'fs')
- w_down: bfloat16 [2, 32, 768, 2048], P('pp', 'ep', 'fs')
- hot_ids: int32 [4], replicated
Outputs:
- output 1: bfloat16 [2, 32, 2048, 1536], P(None, ('pp', 'ep', 'fs'))
- output 2: bfloat16 [2, 32, 768, 2048], P(None, ('pp', 'ep', 'fs'))
- output 3: bfloat16 [2, 4, 2048, 1536], replicated
- output 4: bfloat16 [2, 4, 768, 2048], replicated
All inputs are finite; a program needn't handle non-finite values.
Results may differ from a plain program's by a relative error of at most 0.001.
Values are sent between devices in bfloat16 or wider.
A program may use at most 1 GiB of HBM per device.

v0:
```python
import jax
import jax.numpy as jnp
from jax import lax
from jax.sharding import PartitionSpec as P


def solution(mesh):
    fs_size = mesh.shape["fs"]
    pp_size = mesh.shape["pp"]
    ep_size = mesh.shape["ep"]
    perm_pairs = [(stage_idx * ep_size + col_idx, col_idx * pp_size + stage_idx) for stage_idx in range(pp_size) for col_idx in range(ep_size)]
    in_spec = P("pp", "ep", None, "fs")
    down_spec = P("pp", "ep", "fs", None)
    home_spec = P(None, ("pp", "ep", "fs"), None, None)

    def regroup(shard_in, f_axis):
        lay_local = shard_in.shape[0]
        exp_local = shard_in.shape[1]
        per_dev = exp_local // (fs_size * pp_size)
        split_view = shard_in.reshape((lay_local, pp_size, fs_size, per_dev) + shard_in.shape[2:])
        moved_blk = lax.all_to_all(split_view, "fs", 2, f_axis + 2, tiled=True)
        moved_blk = lax.all_to_all(moved_blk, "pp", 1, 0, tiled=True)
        moved_blk = lax.ppermute(moved_blk, ("pp", "ep"), perm_pairs)
        return moved_blk.reshape((lay_local * pp_size, per_dev) + moved_blk.shape[4:])

    def hot_pick(shard_in, hot_ids, f_axis):
        exp_local = shard_in.shape[1]
        base_id = lax.axis_index("ep") * exp_local
        offset = hot_ids - base_id
        is_held = (offset >= 0) & (offset < exp_local)
        picked = jnp.take(shard_in, jnp.clip(offset, 0, exp_local - 1), axis=1)
        picked = jnp.where(is_held[None, :, None, None], picked, jnp.zeros((), picked.dtype))
        picked = lax.psum(picked, "ep")
        picked = lax.all_gather(picked, "pp", axis=0, tiled=True)
        return lax.all_gather(picked, "fs", axis=f_axis, tiled=True)

    def device_body(w_gate, w_up, w_down, hot_ids):
        gate_home = regroup(w_gate, 3)
        up_home = regroup(w_up, 3)
        down_home = regroup(w_down, 2)
        gate_up = jnp.concatenate([gate_home, up_home], axis=-1)
        hot_gate_up = jnp.concatenate([hot_pick(w_gate, hot_ids, 3), hot_pick(w_up, hot_ids, 3)], axis=-1)
        hot_down = hot_pick(w_down, hot_ids, 2)
        return gate_up, down_home, hot_gate_up, hot_down

    return jax.shard_map(device_body, mesh=mesh, in_specs=(in_spec, in_spec, down_spec, P()), out_specs=(home_spec, home_spec, P(), P()), check_vma=False)
```

profile of v0, /device:TPU:2, one launch (start us, length us, event | category | flops | bytes accessed | tf_op | source)
XLA Modules:
  0.0 2011.6 jit_solution(6160317078907206165)
XLA Ops:
  7.9 8.7 gather_fusion.1
  16.6 8.7 gather_fusion.2
  25.3 8.4 gather_fusion
  33.7 6.4 fusion
  40.1 8.0 fusion.2
  48.2 318.2 %all-reduce.3.cloned.1.call-done = (bf16[1,4,2048,384]{3,2,1,0:T(8,128)(2,1)}, bf16[1,4,2048,384]{3,2,1,0:T(8,128)(2,1)}, bf16[1,4,384,2048]{3,2,1,0:T(8,128)(2,1)}) async-done(((bf16[1,4,2048,384]{3,2,1,0:T(8,128)(2,1)}, bf16[1,4,2048,384]{3,2,1,0:T(8,128)(2,1)}, bf16[1,4,384,2048]{3,2,1,0:T(8,128)(2,1)}), (bf16[1,4,2048,384]{3,2,1,0:T(8,128)(2,1)}, bf16[1,4,2048,384]{3,2,1,0:T(8,128)(2,1)}, ...) | async-done | bytes 18874384 | tf_op jit(solution)/shard_map/psum | solution.py:33
  367.7 152.8 %all-gather.15.cloned.1.call-done = bf16[2,4,384,2048]{3,2,1,0:T(8,128)(2,1)} async-done(((bf16[1,4,384,2048]{3,2,1,0:T(8,128)(2,1)}), bf16[2,4,384,2048]{3,2,1,0:T(8,128)(2,1)}) %all-gather.15.cloned.1.call-update) | async-done | bytes 12582928 | tf_op jit(solution)/shard_map/all_gather | solution.py:34
  520.5 10.5 copy.14
  531.0 8.3 all-to-all-start.2
  539.4 134.2 %all-gather.11.cloned.1.call-done = bf16[2,4,2048,384]{3,2,1,0:T(8,128)(2,1)} async-done(((bf16[1,4,2048,384]{3,2,1,0:T(8,128)(2,1)}), bf16[2,4,2048,384]{3,2,1,0:T(8,128)(2,1)}) %all-gather.11.cloned.1.call-update) | async-done | bytes 12582928 | tf_op jit(solution)/shard_map/all_gather | solution.py:34
  673.6 10.5 copy.11
  684.0 8.3 all-to-all-start
  692.4 10.8 copy.17
  703.1 126.2 %all-to-all-done = bf16[1,2,2,2,2048,384]{5,4,3,1,0,2:T(8,128)(2,1)} async-done(((bf16[1,2,2,2,2048,384]{5,4,3,1,0,2:T(8,128)(2,1)}), bf16[1,2,2,2,2048,384]{5,4,3,1,0,2:T(8,128)(2,1)}, u32[]{:S(2)}, u32[]{:S(2)}) %all-to-all-start) | async-done | bytes 12582944 | tf_op jit(solution)/shard_map/all_to_all | solution.py:21
  829.4 8.4 all-to-all-start.4
  837.7 16.6 copy.15
  854.3 16.6 copy.16
  870.9 229.0 %all-to-all-done.4 = bf16[1,2,2,2,384,2048]{5,4,3,1,0,2:T(8,128)(2,1)} async-done(((bf16[1,2,2,2,384,2048]{5,4,3,1,0,2:T(8,128)(2,1)}), bf16[1,2,2,2,384,2048]{5,4,3,1,0,2:T(8,128)(2,1)}, u32[]{:S(2)}, u32[]{:S(2)}) %all-to-all-start.4) | async-done | bytes 12582944 | tf_op jit(solution)/shard_map/all_to_all | solution.py:21
  1099.9 8.4 all-to-all-start.3
  1108.3 10.8 copy.18
  1119.1 120.5 %all-to-all-done.3 = bf16[1,2,1,2,2048,768]{5,4,3,2,0,1:T(8,128)(2,1)} async-done(((bf16[1,2,1,2,2048,768]{5,4,3,2,0,1:T(8,128)(2,1)}), bf16[1,2,1,2,2048,768]{5,4,3,2,0,1:T(8,128)(2,1)}, u32[]{:S(2)}, u32[]{:S(2)}) %all-to-all-start.3) | async-done | bytes 12582944 | tf_op jit(solution)/shard_map/all_to_all | solution.py:22
  1239.6 8.4 all-to-all-start.5
  1248.7 16.6 copy.12
  1265.4 16.6 copy.13
  1282.0 96.5 %all-to-all-done.5 = bf16[1,2,1,2,768,2048]{5,4,3,2,0,1:T(8,128)(2,1)} async-done(((bf16[1,2,1,2,768,2048]{5,4,3,2,0,1:T(8,128)(2,1)}), bf16[1,2,1,2,768,2048]{5,4,3,2,0,1:T(8,128)(2,1)}, u32[]{:S(2)}, u32[]{:S(2)}) %all-to-all-start.5) | async-done | bytes 12582944 | tf_op jit(solution)/shard_map/all_to_all | solution.py:22
  1378.5 8.4 all-to-all-start.1
  1392.7 393.5 %all-to-all-done.1 = bf16[1,2,1,2,2048,768]{5,4,3,2,0,1:T(8,128)(2,1)} async-done(((bf16[1,2,1,2,2048,768]{5,4,3,2,0,1:T(8,128)(2,1)}), bf16[1,2,1,2,2048,768]{5,4,3,2,0,1:T(8,128)(2,1)}, u32[]{:S(2)}, u32[]{:S(2)}) %all-to-all-start.1) | async-done | bytes 12582944 | tf_op jit(solution)/shard_map/all_to_all | solution.py:22
  1788.4 137.5 %collective-permute-done = bf16[2,1,1,2,2048,768]{5,4,3,0,2,1:T(8,128)(2,1)} collective-permute-done((bf16[2,1,1,2,2048,768]{5,4,3,0,2,1:T(8,128)(2,1)}, bf16[2,1,1,2,2048,768]{5,4,3,0,2,1:T(8,128)(2,1)}, u32[]{:S(2)}, u32[]{:S(2)}) %collective-permute-start) | collective-permute-done | bytes 12582944 | tf_op jit(solution)/shard_map/ppermute | solution.py:23
  1925.9 20.4 %pad_maximum_fusion.1 = bf16[2,2,2048,1536]{3,2,1,0:T(8,128)(2,1)} fusion(bf16[2,2,2048,768]{3,2,1,0:T(8,128)(2,1)} %bitcast.11, bf16[2,2,2048,768]{3,2,1,0:T(8,128)(2,1)} %bitcast.5), kind=kLoop, calls=%fused_computation.4 | loop fusion | flops 50331648 | bytes 50331648 | tf_op jit(solution)/shard_map/concatenate | solution.py:41
  1946.3 33.1 %pad_maximum_fusion = bf16[2,4,2048,1536]{3,2,1,0:T(8,128)(2,1)} fusion(bf16[2,4,2048,768]{3,2,1,0:T(8,128)(2,1)} %all-gather.13.cloned.1.call-done, bf16[2,4,2048,768]{3,2,1,0:T(8,128)(2,1)} %all-gather.9.cloned.1.call-done), kind=kLoop, calls=%fused_computation.3 | loop fusion | flops 100663296 | bytes 100663296 | tf_op jit(solution)/shard_map/concatenate | solution.py:42
  1979.3 11.4 copy.25
  1995.8 8.9 copy.26
  (33 shorter events, 16.0 us)
Async XLA Ops:
  7.2 359.2 %all-reduce.3.cloned.1.call-start = ((), (), s32[]{:S(2)}) async-start(), calls=%async_computation.12 | async-start | bytes 37748736 | tf_op jit(solution)/shard_map/psum | solution.py:33
  25.3 14.8 slice-start
  33.7 6.4 slice-start.1
  48.2 472.4 %all-gather.15.cloned.1.call-start = ((), (), s32[]{:S(2)}) async-start(), calls=%async_computation.10 | async-start | bytes 18874368 | tf_op jit(solution)/shard_map/all_gather | solution.py:34
  366.4 307.2 %all-gather.11.cloned.1.call-start = ((), (), s32[]{:S(2)}) async-start(), calls=%async_computation.8 | async-start | bytes 18874368 | tf_op jit(solution)/shard_map/all_gather | solution.py:34
  367.1 880.9 %all-gather.7.cloned.1.call-start = ((), (), s32[]{:S(2)}) async-start(), calls=%async_computation.6 | async-start | bytes 18874368 | tf_op jit(solution)/shard_map/all_gather | solution.py:34
  367.7 1578.6 %all-gather.17.cloned.1.call-start = ((), (), s32[]{:S(2)}) async-start(), calls=%async_computation.11 | async-start | bytes 37748736 | tf_op jit(solution)/shard_map/all_gather | solution.py:35
  531.0 153.1 %all-to-all-start.2 = ((bf16[1,2,2,2,2048,384]{5,4,3,1,0,2:T(8,128)(2,1)}), bf16[1,2,2,2,2048,384]{5,4,3,1,0,2:T(8,128)(2,1)}, u32[]{:S(2)}, u32[]{:S(2)}) async-start(bf16[1,2,2,2,2048,384]{5,4,3,1,0,2:T(8,128)(2,1)} %copy.14), calls=%async_computation.2 | async-start | bytes 25165824 | tf_op jit(solution)/shard_map/all_to_all | solution.py:21
  539.3 1406.9 %all-gather.13.cloned.1.call-start = ((), (), s32[]{:S(2)}) async-start(), calls=%async_computation.9 | async-start | bytes 37748736 | tf_op jit(solution)/shard_map/all_gather | solution.py:35
  684.0 145.3 %all-to-all-start = ((bf16[1,2,2,2,2048,384]{5,4,3,1,0,2:T(8,128)(2,1)}), bf16[1,2,2,2,2048,384]{5,4,3,1,0,2:T(8,128)(2,1)}, u32[]{:S(2)}, u32[]{:S(2)}) async-start(bf16[1,2,2,2,2048,384]{5,4,3,1,0,2:T(8,128)(2,1)} %copy.11), calls=%async_computation | async-start | bytes 25165824 | tf_op jit(solution)/shard_map/all_to_all | solution.py:21
  829.4 270.6 %all-to-all-start.4 = ((bf16[1,2,2,2,384,2048]{5,4,3,1,0,2:T(8,128)(2,1)}), bf16[1,2,2,2,384,2048]{5,4,3,1,0,2:T(8,128)(2,1)}, u32[]{:S(2)}, u32[]{:S(2)}) async-start(bf16[1,2,2,2,384,2048]{5,4,3,1,0,2:T(8,128)(2,1)} %copy.17), calls=%async_computation.4 | async-start | bytes 25165824 | tf_op jit(solution)/shard_map/all_to_all | solution.py:21
  1099.9 139.6 %all-to-all-start.3 = ((bf16[1,2,1,2,2048,768]{5,4,3,2,0,1:T(8,128)(2,1)}), bf16[1,2,1,2,2048,768]{5,4,3,2,0,1:T(8,128)(2,1)}, u32[]{:S(2)}, u32[]{:S(2)}) async-start(bf16[1,2,1,2,2048,768]{5,4,3,2,0,1:T(8,128)(2,1)} %copy.16), calls=%async_computation.3 | async-start | bytes 25165824 | tf_op jit(solution)/shard_map/all_to_all | solution.py:22
  1239.6 138.9 %all-to-all-start.5 = ((bf16[1,2,1,2,768,2048]{5,4,3,2,0,1:T(8,128)(2,1)}), bf16[1,2,1,2,768,2048]{5,4,3,2,0,1:T(8,128)(2,1)}, u32[]{:S(2)}, u32[]{:S(2)}) async-start(bf16[1,2,1,2,768,2048]{5,4,3,2,0,1:T(8,128)(2,1)} %bitcast.41), calls=%async_computation.5 | async-start | bytes 25165824 | tf_op jit(solution)/shard_map/all_to_all | solution.py:22
  1248.0 698.3 %all-gather.9.cloned.1.call-start = ((), (), s32[]{:S(2)}) async-start(), calls=%async_computation.7 | async-start | bytes 37748736 | tf_op jit(solution)/shard_map/all_gather | solution.py:35
  1378.5 407.7 %all-to-all-start.1 = ((bf16[1,2,1,2,2048,768]{5,4,3,2,0,1:T(8,128)(2,1)}), bf16[1,2,1,2,2048,768]{5,4,3,2,0,1:T(8,128)(2,1)}, u32[]{:S(2)}, u32[]{:S(2)}) async-start(bf16[1,2,1,2,2048,768]{5,4,3,2,0,1:T(8,128)(2,1)} %copy.13), calls=%async_computation.1 | async-start | bytes 25165824 | tf_op jit(solution)/shard_map/all_to_all | solution.py:22
  1386.8 401.6 %collective-permute-start.2 = (bf16[2,1,1,2,768,2048]{5,4,3,0,2,1:T(8,128)(2,1)}, bf16[2,1,1,2,768,2048]{5,4,3,0,2,1:T(8,128)(2,1)}, u32[]{:S(2)}, u32[]{:S(2)}) collective-permute-start(bf16[2,1,1,2,768,2048]{5,4,3,0,2,1:T(8,128)(2,1)} %bitcast.17), channel_id=1, source_target_pairs={{0,0},{1,2},{2,4},{3,6},{4,1},{5,3},{6,5},{7,7},{8,8},{9,10},{10,1... | collective-permute-start | bytes 37748744 | tf_op jit(solution)/shard_map/ppermute | solution.py:23
  1390.7 397.7 %collective-permute-start.1 = (bf16[2,1,1,2,2048,768]{5,4,3,0,2,1:T(8,128)(2,1)}, bf16[2,1,1,2,2048,768]{5,4,3,0,2,1:T(8,128)(2,1)}, u32[]{:S(2)}, u32[]{:S(2)}) collective-permute-start(bf16[2,1,1,2,2048,768]{5,4,3,0,2,1:T(8,128)(2,1)} %bitcast.10), channel_id=1, source_target_pairs={{0,0},{1,2},{2,4},{3,6},{4,1},{5,3},{6,5},{7,7},{8,8},{9,10},{10,1... | collective-permute-start | bytes 37748744 | tf_op jit(solution)/shard_map/ppermute | solution.py:23
  1786.2 139.7 %collective-permute-start = (bf16[2,1,1,2,2048,768]{5,4,3,0,2,1:T(8,128)(2,1)}, bf16[2,1,1,2,2048,768]{5,4,3,0,2,1:T(8,128)(2,1)}, u32[]{:S(2)}, u32[]{:S(2)}) collective-permute-start(bf16[2,1,1,2,2048,768]{5,4,3,0,2,1:T(8,128)(2,1)} %bitcast.4), channel_id=1, source_target_pairs={{0,0},{1,2},{2,4},{3,6},{4,1},{5,3},{6,5},{7,7},{8,8},{9,10},{10,1... | collective-permute-start | bytes 37748744 | tf_op jit(solution)/shard_map/ppermute | solution.py:23
  1979.3 16.5 copy-start
Sparse Core Ops, SparseCore 0:
  48.3 318.0 all-reduce.2
  367.9 152.5 all-gather.14
  522.0 151.4 all-gather.10
  674.9 151.4 all-gather.6
  827.8 415.8 all-gather.16
  1245.1 293.3 all-gather.12
  1540.1 294.2 all-gather.8
where the time goes:
time: 2040 us; the launch traced here: 2010 us
  waiting for transfers between devices  1710 us (84%)
  local copies, waits for them, and re-layouts  160 us (8%)
  other arithmetic  68.5 us (3%)
  starting transfers between devices  58.5 us (3%)
    all_to_all x3, waiting for transfers between devices, regroup(): moved_blk = lax.all_to_all(moved_blk, 'pp', 1, 0, tiled=True)  610 us
    all_to_all x3, waiting for transfers between devices, regroup(): moved_blk = lax.all_to_all(split_view, 'fs', 2, f_axis + 2, tiled=True)  355 us
    psum x1, waiting for transfers between devices, hot_pick(): picked = lax.psum(picked, 'ep')  318 us
    all_gather x3, waiting for transfers between devices, hot_pick(): picked = lax.all_gather(picked, 'pp', axis=0, tiled=True)  287 us
    ppermute x3, waiting for transfers between devices, regroup(): moved_blk = lax.ppermute(moved_blk, ('pp', 'ep'), perm_pairs)  137 us
    all_to_all x5, local copies, waits for them, and re-layouts, regroup(): moved_blk = lax.all_to_all(split_view, 'fs', 2, f_axis + 2, tiled=True)  77.2 us
  transfers between devices with their start and end apart: 16, of which 9 were waited for; matrix products, arithmetic and copies ran while one was open for 6% of the time, Pallas kernels for 0%

commit v1 on v0

v1 whole, which is shorter than its diff:
```python
import functools

import jax
import jax.numpy as jnp
from jax import lax
from jax.experimental import pallas as pl
from jax.experimental.pallas import tpu as pltpu
from jax.sharding import PartitionSpec as P

MESH = pl.DeviceIdType.MESH
ANY = pl.BlockSpec(memory_space=pl.ANY)


def pick_kernel(off_ref, g_ref, u_ref, d_ref, pg_ref, pu_ref, pd_ref):
    pg_ref[...] = g_ref[0]
    pu_ref[...] = u_ref[0]
    pd_ref[...] = d_ref[0]


def pick_hot(w_gate, w_up, w_down, offset):
    hot = offset.shape[0]
    _, _, d_model, f_loc = w_gate.shape
    take_in = lambda h, off: (0, off[h], 0, 0)
    put = lambda h, off: (h, 0, 0)
    shape_in = jax.ShapeDtypeStruct((hot, d_model, f_loc), w_gate.dtype)
    shape_down = jax.ShapeDtypeStruct((hot, f_loc, d_model), w_gate.dtype)
    return pl.pallas_call(
        pick_kernel,
        grid_spec=pltpu.PrefetchScalarGridSpec(
            num_scalar_prefetch=1,
            grid=(hot,),
            in_specs=[
                pl.BlockSpec((1, 1, d_model, f_loc), take_in),
                pl.BlockSpec((1, 1, d_model, f_loc), take_in),
                pl.BlockSpec((1, 1, f_loc, d_model), take_in),
            ],
            out_specs=[
                pl.BlockSpec((1, d_model, f_loc), put),
                pl.BlockSpec((1, d_model, f_loc), put),
                pl.BlockSpec((1, f_loc, d_model), put),
            ],
        ),
        out_shape=[shape_in, shape_in, shape_down],
    )(offset, w_gate, w_up, w_down)


def move_kernel(
    owner_ref, wg, wu, wd, pg, pu, pd, o13, o2, h13, h2,
    own13, own2, par13, par2, far13, far2,
    rg_send, rg_recv, loc_sem, dd_send, dd_recv, x_send, x_recv,
    n_send, n_recv, q_send, q_recv, w_sem,
):
    z = lax.axis_index("fs")
    y = lax.axis_index("pp")
    ep = lax.axis_index("ep")
    x, c = ep // 2, ep % 2
    d_model, f_loc = wg.shape[2], wg.shape[3]
    f_all = f_loc * 2
    partner = (z, y, x * 2 + 1 - c)
    x_nbr = (z, y, (1 - x) * 2 + c)
    y_nbr = (z, 1 - y, ep)
    z_nbr = (1 - z, y, ep)

    def cols(half, up):
        return pl.ds(pl.multiple_of(half * f_loc + up * f_all, 128), f_loc)

    def remote(src, dst, send, recv, dev):
        return pltpu.make_async_remote_copy(
            src_ref=src, dst_ref=dst, send_sem=send, recv_sem=recv, device_id=dev, device_id_type=MESH
        )

    def vmem(b13, b2, k):
        return b2.at[k // 3] if k % 3 == 2 else b13.at[(k // 3) * 2 + k % 3]

    def picked(h, w):
        return (pg, pu, pd)[w].at[h]

    def hot_at(h, lay, half, w):
        if w == 2:
            return h2.at[lay, h, pl.ds(pl.multiple_of(half * f_loc, 128), f_loc)]
        return h13.at[lay, h, :, cols(half, w)]

    stays = (x == y) & (c == x)

    def home_refs(j, i, b0, w):
        b1, b2 = (z + i) % 2, (c + j) % 2
        src = (wg, wu, wd)[w].at[0, 4 * b2 + 2 * b1 + b0]
        if w == 2:
            dst = o2.at[y, b0, pl.ds(pl.multiple_of(z * f_loc, 128), f_loc)]
        else:
            dst = o13.at[y, b0, :, cols(z, w)]
        return src, dst, rg_recv.at[w, b0, y * 2 + z], (b1, x, c * 2 + b2)

    def home_copy(j, i, b0, w):
        src, dst, recv, dev = home_refs(j, i, b0, w)
        return remote(src, dst, rg_send.at[w, 4 * j + 2 * i + b0], recv, dev)

    def home_start(j, i, b0, w):
        if (j, i) != (0, 0):
            home_copy(j, i, b0, w).start()
            return

        @pl.when(stays)
        def _():
            src, dst, recv, _ = home_refs(j, i, b0, w)
            pltpu.make_async_copy(src, dst, recv).start()

        @pl.when(jnp.logical_not(stays))
        def _():
            home_copy(j, i, b0, w).start()

    def home_sent(j, i, b0, w):
        if (j, i) != (0, 0):
            home_copy(j, i, b0, w).wait_send()
            return

        @pl.when(jnp.logical_not(stays))
        def _():
            home_copy(j, i, b0, w).wait_send()

    homes = [(j, i, b0, w) for b0 in range(2) for w in range(3) for j in range(2) for i in range(2)]

    CH = range(6)
    dd = [remote(picked(2 * (1 - c) + k // 3, k % 3), vmem(par13, par2, k), dd_send.at[k], dd_recv.at[k], partner) for k in CH]
    own = [pltpu.make_async_copy(picked(2 * c + k // 3, k % 3), vmem(own13, own2, k), loc_sem.at[k]) for k in CH]
    xs = [remote(vmem(own13, own2, k), vmem(far13, far2, k), x_send.at[k], x_recv.at[k], x_nbr) for k in CH]

    def choose(take_a, a, b, out):
        rows = a.shape[0] // 8

        def body(i, carry):
            at = pl.ds(pl.multiple_of(i * rows, 16), rows)
            out[at, :] = jnp.where(take_a, a[at, :], b[at, :])
            return carry

        lax.fori_loop(0, 8, body, 0)

    for k in CH:
        own[k].start()
        dd[k].start()
    for b in homes[:2]:
        home_start(*b)
    for k in CH:
        own[k].wait()
        dd[k].wait_recv()
        owner = owner_ref[2 * c + k // 3]
        choose(owner % 2 == c, vmem(own13, own2, k), vmem(par13, par2, k), vmem(own13, own2, k))
        if k > 0:
            xs[k - 1].start()
    for b in homes[2:4]:
        home_start(*b)
    xs[5].start()
    for b in homes[4:]:
        home_start(*b)

    def hot_of(k):
        return 2 * c + k // 3

    def fan(k):
        src, w = vmem(par13, par2, k), k % 3
        dst = hot_at(hot_of(k), y, z, w)
        return (
            remote(src, dst, n_send.at[0, k], n_recv.at[0, k], y_nbr),
            remote(src, dst, n_send.at[1, k], n_recv.at[1, k], z_nbr),
            remote(src, dst, q_send.at[0, k], q_recv.at[0, k], partner),
            pltpu.make_async_copy(src, dst, w_sem.at[k]),
        )

    def from_y(k):
        at = hot_at(hot_of(k), 1 - y, z, k % 3)
        return at, remote(at, at, q_send.at[1, k], q_recv.at[1, k], partner)

    def from_z(k):
        at = hot_at(hot_of(k), y, 1 - z, k % 3)
        return at, remote(at, at, q_send.at[2, k], q_recv.at[2, k], partner)

    def onward(k):
        if k % 2 == 0:
            at = hot_at(hot_of(k), 1 - y, z, k % 3)
            return remote(at, at, n_send.at[2, k], n_recv.at[2, k], z_nbr)
        at = hot_at(hot_of(k), y, 1 - z, k % 3)
        return remote(at, at, n_send.at[2, k], n_recv.at[2, k], y_nbr)

    def from_diag(k):
        at = hot_at(hot_of(k), 1 - y, 1 - z, k % 3)
        return at, remote(at, at, q_send.at[3, k], q_recv.at[3, k], partner)

    def landed(at, sem):
        pltpu.make_async_copy(at, at, sem).wait()

    for k in CH:
        xs[k].wait_recv()
        owner = owner_ref[2 * c + k // 3]
        choose(owner // 2 == x, vmem(own13, own2, k), vmem(far13, far2, k), vmem(par13, par2, k))
        if k > 0:
            for copy in fan(k - 1):
                copy.start()
    for k in CH:
        xs[k].wait_send()
    for copy in fan(5):
        copy.start()
    for k in CH:
        at, pass_on = from_y(k)
        landed(at, n_recv.at[0, k])
        if k % 2 == 0:
            onward(k).start()
        pass_on.start()
        at, pass_on = from_z(k)
        landed(at, n_recv.at[1, k])
        if k % 2 == 1:
            onward(k).start()
        pass_on.start()
    for k in CH:
        at, pass_on = from_diag(k)
        landed(at, n_recv.at[2, k])
        pass_on.start()

    for k in CH:
        dd[k].wait_send()
        to_y, to_z, to_p, to_self = fan(k)
        to_y.wait_send()
        to_z.wait_send()
        to_p.wait_send()
        to_self.wait()
        onward(k).wait_send()
        from_y(k)[1].wait_send()
        from_z(k)[1].wait_send()
        from_diag(k)[1].wait_send()
    for k in CH:
        h, w = 2 * (1 - c) + k // 3, k % 3
        landed(hot_at(h, y, z, w), q_recv.at[0, k])
        landed(hot_at(h, 1 - y, z, w), q_recv.at[1, k])
        landed(hot_at(h, y, 1 - z, w), q_recv.at[2, k])
        landed(hot_at(h, 1 - y, 1 - z, w), q_recv.at[3, k])
    for b in homes:
        home_sent(*b)
    for w in range(3):
        for b0 in range(2):
            for lay in range(2):
                for half in range(2):
                    if w == 2:
                        at = o2.at[lay, b0, pl.ds(half * f_loc, f_loc)]
                    else:
                        at = o13.at[lay, b0, :, pl.ds(half * f_loc + w * f_all, f_loc)]
                    landed(at, rg_recv.at[w, b0, lay * 2 + half])


def solution(mesh):
    fs_size, pp_size, ep_size = mesh.shape["fs"], mesh.shape["pp"], mesh.shape["ep"]
    in_spec = P("pp", "ep", None, "fs")
    down_spec = P("pp", "ep", "fs", None)
    home_spec = P(None, ("pp", "ep", "fs"), None, None)

    def device_body(w_gate, w_up, w_down, hot_ids):
        dtype = w_gate.dtype
        lay, exp_local, d_model, f_loc = w_gate.shape
        hot = hot_ids.shape[0]
        layers, f_all = lay * pp_size, f_loc * fs_size
        home = exp_local // (fs_size * pp_size)
        offset = jnp.clip(hot_ids - lax.axis_index("ep") * exp_local, 0, exp_local - 1)
        owner = hot_ids // exp_local
        picked = pick_hot(w_gate, w_up, w_down, offset)
        dma = pltpu.SemaphoreType.DMA
        buf13 = pltpu.VMEM((4, d_model, f_loc), dtype)
        buf2 = pltpu.VMEM((2, f_loc, d_model), dtype)
        return pl.pallas_call(
            move_kernel,
            out_shape=[
                jax.ShapeDtypeStruct((layers, home, d_model, 2 * f_all), dtype),
                jax.ShapeDtypeStruct((layers, home, f_all, d_model), dtype),
                jax.ShapeDtypeStruct((layers, hot, d_model, 2 * f_all), dtype),
                jax.ShapeDtypeStruct((layers, hot, f_all, d_model), dtype),
            ],
            in_specs=[pl.BlockSpec(memory_space=pltpu.SMEM)] + [ANY] * 6,
            out_specs=[ANY] * 4,
            scratch_shapes=[
                buf13, buf2, buf13, buf2, buf13, buf2,
                dma((3, 8)), dma((3, 2, 4)), dma((6,)), dma((6,)), dma((6,)), dma((6,)), dma((6,)),
                dma((3, 6)), dma((3, 6)), dma((4, 6)), dma((4, 6)), dma((6,)),
            ],
            compiler_params=pltpu.CompilerParams(has_side_effects=True, vmem_limit_bytes=48 * 1024 * 1024),
        )(owner, w_gate, w_up, w_down, *picked)

    return jax.shard_map(
        device_body,
        mesh=mesh,
        in_specs=(in_spec, in_spec, down_spec, P()),
        out_specs=(home_spec, home_spec, P(), P()),
        check_vma=False,
    )
```

time: 2040 us -> 880 us (0.43); the launches traced: 2010 us -> 879 us
  waiting for transfers between devices: 1710 us -> 0 us
  Pallas kernels: 0 us -> 797 us
  local copies, waits for them, and re-layouts: 160 us -> 81 us
  other arithmetic: 68.5 us -> 1.17 us
  starting transfers between devices: 58.5 us -> 0 us
    all_to_all x6 -> x0, waiting for transfers between devices: 966 us -> none  [the longest x3 610 us: regroup(): moved_blk = lax.all_to_all(moved_blk, 'pp', 1, 0, tiled=True)]
    pallas_call x0 -> x2, Pallas kernels: none -> 797 us  [the longest x1 783 us: device_body(): pl.pallas_call(move_kernel, out_shape=[jax.ShapeDtypeStruct((layers, home...]
    psum x1 -> x0, waiting for transfers between devices: 318 us -> none  [hot_pick(): picked = lax.psum(picked, 'ep')]
    all_gather x6 -> x0, waiting for transfers between devices: 287 us -> none  [the longest x3 287 us: hot_pick(): picked = lax.all_gather(picked, 'pp', axis=0, tiled=True)]
    ppermute x3 -> x0, waiting for transfers between devices: 137 us -> none  [regroup(): moved_blk = lax.ppermute(moved_blk, ('pp', 'ep'), perm_pairs)]
    all_to_all x5 -> x0, local copies, waits for them, and re-layouts: 77.2 us -> none  [regroup(): moved_blk = lax.all_to_all(split_view, 'fs', 2, f_axis + 2, tiled=True)]
    unnamed x8 -> x6, local copies, waits for them, and re-layouts: 25.4 us -> 81 us
    concatenate x2 -> x0, other arithmetic: 53.4 us -> none  [the longest x1 33.1 us: device_body(): jnp.concatenate([hot_pick(w_gate, hot_ids, 3), hot_pick(w_up, hot_ids, 3)...]
  transfers between devices with their start and end apart: 16 -> 0, of which waited for: 9 -> 0; matrix products, arithmetic and copies ran while one was open for 6% -> 0% of each run, Pallas kernels for 0% -> 0%
where the time goes in v1:
time: 880 us; the launch traced here: 879 us
  Pallas kernels  797 us (91%)
  local copies, waits for them, and re-layouts  81 us (9%)
    pallas_call x1, Pallas kernels, device_body(): pl.pallas_call(move_kernel, out_shape=[jax.ShapeDtypeStruct((layers, home...  783 us
    unnamed x6, local copies, waits for them, and re-layouts  81 us

profile of v1, /device:TPU:2, one launch (start us, length us, event | category | flops | bytes accessed | tf_op | source)
XLA Modules:
  0.0 879.4 jit_solution(7892916290280891010)
XLA Ops:
  0.6 1.2 subtract_clamp_fusion
  1.8 13.3 %shard_map.75 = (bf16[4,2048,384]{2,1,0:T(8,128)(2,1)}, bf16[4,2048,384]{2,1,0:T(8,128)(2,1)}, bf16[4,384,2048]{2,1,0:T(8,128)(2,1)}) custom-call(s32[4]{0:T(128)} %get-tuple-element.10.off_ref, bf16[1,8,2048,384]{3,2,1,0:T(8,128)(2,1)} %wg.1, bf16[1,8,2048,384]{3,2,1,0:T(8,128)(2,1)} %wu.1, bf16[1,8,384,2048]{3,2,1,0:T(8,128)(2,1)} %wd.1), custom_call_target="tpu_custom_call" | custom-call | tf_op jit(solution)/shard_map/pallas_call | solution.py:27
  15.1 783.3 %shard_map.76 = (bf16[2,2,2048,1536]{3,2,1,0:T(8,128)(2,1)}, bf16[2,2,768,2048]{3,2,1,0:T(8,128)(2,1)}, bf16[2,4,2048,1536]{3,2,1,0:T(8,128)(2,1)}, bf16[2,4,768,2048]{3,2,1,0:T(8,128)(2,1)}) custom-call(s32[4]{0:T(128)S(1)} %get-tuple-element.11.owner_ref, bf16[1,8,2048,384]{3,2,1,0:T(8,128)(2,1)} %wg.1, bf16[1,8,2048,384]{3,2,1,0:T(8,128)(2,1)} %wu.1, ...), custom_call_target="tpu_custom_call" | custom-call | tf_op jit(solution)/shard_map/pallas_call | solution.py:266
  798.4 0.0 copy-start
  798.4 21.4 %copy.12 = bf16[2,2,2048,1536]{3,2,1,0:T(8,128)(2,1)} copy(bf16[2,2,2048,1536]{3,2,1,0:T(8,128)(2,1)} %get-tuple-element.16) | data formatting | bytes 50331648
  819.9 0.0 copy-done
  819.9 4.8 copy.13
  824.7 33.7 %copy.14 = bf16[2,4,2048,1536]{3,2,1,0:T(8,128)(2,1)} copy(bf16[2,4,2048,1536]{3,2,1,0:T(8,128)(2,1)} %get-tuple-element.18) | data formatting | bytes 100663296
  858.3 21.1 %copy.15 = bf16[2,4,768,2048]{3,2,1,0:T(8,128)(2,1)} copy(bf16[2,4,768,2048]{3,2,1,0:T(8,128)(2,1)} %get-tuple-element.19) | data formatting | bytes 50331648
Async XLA Ops:
  798.4 21.5 %copy-start = (bf16[2,2,768,2048]{3,2,1,0:T(8,128)(2,1)S(1)}, bf16[2,2,768,2048]{3,2,1,0:T(8,128)(2,1)}, u32[]{:S(2)}) copy-start(bf16[2,2,768,2048]{3,2,1,0:T(8,128)(2,1)} %get-tuple-element.17) | copy-start | bytes 37748740

commit v2 on v1

--- a/solution.py
+++ b/solution.py
@@ -48,7 +48,7 @@
     owner_ref, wg, wu, wd, pg, pu, pd, o13, o2, h13, h2,
     own13, own2, par13, par2, far13, far2,
     rg_send, rg_recv, loc_sem, dd_send, dd_recv, x_send, x_recv,
-    n_send, n_recv, q_send, q_recv, w_sem,
+    n_send, n_recv, f_send, q_send, q_recv, w_sem,
 ):
     z = lax.axis_index("fs")
     y = lax.axis_index("pp")
@@ -120,6 +120,12 @@
 
     homes = [(j, i, b0, w) for b0 in range(2) for w in range(3) for j in range(2) for i in range(2)]
 
+    waiting = list(homes)
+
+    def issue(count):
+        for _ in range(count):
+            home_start(*waiting.pop(0))
+
     CH = range(6)
     dd = [remote(picked(2 * (1 - c) + k // 3, k % 3), vmem(par13, par2, k), dd_send.at[k], dd_recv.at[k], partner) for k in CH]
     own = [pltpu.make_async_copy(picked(2 * c + k // 3, k % 3), vmem(own13, own2, k), loc_sem.at[k]) for k in CH]
@@ -138,8 +144,7 @@
     for k in CH:
         own[k].start()
         dd[k].start()
-    for b in homes[:2]:
-        home_start(*b)
+    issue(2)
     for k in CH:
         own[k].wait()
         dd[k].wait_recv()
@@ -147,11 +152,9 @@
         choose(owner % 2 == c, vmem(own13, own2, k), vmem(par13, par2, k), vmem(own13, own2, k))
         if k > 0:
             xs[k - 1].start()
-    for b in homes[2:4]:
-        home_start(*b)
+    issue(1)
     xs[5].start()
-    for b in homes[4:]:
-        home_start(*b)
+    issue(3)
 
     def hot_of(k):
         return 2 * c + k // 3
@@ -188,32 +191,48 @@
     def landed(at, sem):
         pltpu.make_async_copy(at, at, sem).wait()
 
-    for k in CH:
-        xs[k].wait_recv()
-        owner = owner_ref[2 * c + k // 3]
-        choose(owner // 2 == x, vmem(own13, own2, k), vmem(far13, far2, k), vmem(par13, par2, k))
-        if k > 0:
-            for copy in fan(k - 1):
+    def comes_here(k):
+        return x == k // 2
+
+    def across(k):
+        at = hot_at(hot_of(k), 1 - y, 1 - z, k % 3)
+        return remote(at, at, f_send.at[k], n_recv.at[2, k], x_nbr)
+
+    def onward_do(k, what):
+        if k < 4:
+            pl.when(comes_here(k))(lambda: what(onward(k)))
+        else:
+            what(onward(k))
+
+    for s in range(10):
+        if s < 6:
+            xs[s].wait_recv()
+            owner = owner_ref[2 * c + s // 3]
+            choose(owner // 2 == x, vmem(own13, own2, s), vmem(far13, far2, s), vmem(par13, par2, s))
+        if 1 <= s <= 6:
+            for copy in fan(s - 1):
                 copy.start()
-    for k in CH:
-        xs[k].wait_send()
-    for copy in fan(5):
-        copy.start()
-    for k in CH:
-        at, pass_on = from_y(k)
-        landed(at, n_recv.at[0, k])
-        if k % 2 == 0:
-            onward(k).start()
-        pass_on.start()
-        at, pass_on = from_z(k)
-        landed(at, n_recv.at[1, k])
-        if k % 2 == 1:
-            onward(k).start()
-        pass_on.start()
-    for k in CH:
-        at, pass_on = from_diag(k)
-        landed(at, n_recv.at[2, k])
-        pass_on.start()
+        if s < 9:
+            issue(2)
+        k = s - 2
+        if 0 <= k < 6:
+            at, pass_on = from_y(k)
+            landed(at, n_recv.at[0, k])
+            if k % 2 == 0:
+                onward_do(k, lambda copy: copy.start())
+            pass_on.start()
+            at, pass_on = from_z(k)
+            landed(at, n_recv.at[1, k])
+            if k % 2 == 1:
+                onward_do(k, lambda copy: copy.start())
+            pass_on.start()
+        k = s - 4
+        if 0 <= k < 6:
+            at, pass_on = from_diag(k)
+            landed(at, n_recv.at[2, k])
+            if k < 4:
+                pl.when(comes_here(k))(lambda: across(k).start())
+            pass_on.start()
 
     for k in CH:
         dd[k].wait_send()
@@ -222,7 +241,10 @@
         to_z.wait_send()
         to_p.wait_send()
         to_self.wait()
-        onward(k).wait_send()
+        xs[k].wait_send()
+        onward_do(k, lambda copy: copy.wait_send())
+        if k < 4:
+            pl.when(comes_here(k))(lambda: across(k).wait_send())
         from_y(k)[1].wait_send()
         from_z(k)[1].wait_send()
         from_diag(k)[1].wait_send()
@@ -276,7 +298,7 @@
             scratch_shapes=[
                 buf13, buf2, buf13, buf2, buf13, buf2,
                 dma((3, 8)), dma((3, 2, 4)), dma((6,)), dma((6,)), dma((6,)), dma((6,)), dma((6,)),
-                dma((3, 6)), dma((3, 6)), dma((4, 6)), dma((4, 6)), dma((6,)),
+                dma((3, 6)), dma((3, 6)), dma((4,)), dma((4, 6)), dma((4, 6)), dma((6,)),
             ],
             compiler_params=pltpu.CompilerParams(has_side_effects=True, vmem_limit_bytes=48 * 1024 * 1024),
         )(owner, w_gate, w_up, w_down, *picked)

time: 880 us -> 940 us (1.068)
  Pallas kernels: 797 us -> 856 us
    pallas_call x1, Pallas kernels: 783 us -> 846 us  [device_body(): pl.pallas_call(move_kernel, out_shape=[jax.ShapeDtypeStruct((layers, home...]
where the time goes in v2:
time: 940 us; the launch traced here: 939 us
  Pallas kernels  856 us (91%)
  local copies, waits for them, and re-layouts  81 us (9%)
    pallas_call x1, Pallas kernels, device_body(): pl.pallas_call(move_kernel, out_shape=[jax.ShapeDtypeStruct((layers, home...  846 us
    unnamed x6, local copies, waits for them, and re-layouts  81 us

profile of v2, /device:TPU:2, one launch (start us, length us, event | category | flops | bytes accessed | tf_op | source)
XLA Modules:
  0.0 939.0 jit_solution(3773018448313650194)
XLA Ops:
  0.6 1.2 subtract_clamp_fusion
  1.8 9.9 %shard_map.75 = (bf16[4,2048,384]{2,1,0:T(8,128)(2,1)}, bf16[4,2048,384]{2,1,0:T(8,128)(2,1)}, bf16[4,384,2048]{2,1,0:T(8,128)(2,1)}) custom-call(s32[4]{0:T(128)} %get-tuple-element.10.off_ref, bf16[1,8,2048,384]{3,2,1,0:T(8,128)(2,1)} %wg.1, bf16[1,8,2048,384]{3,2,1,0:T(8,128)(2,1)} %wu.1, bf16[1,8,384,2048]{3,2,1,0:T(8,128)(2,1)} %wd.1), custom_call_target="tpu_custom_call" | custom-call | tf_op jit(solution)/shard_map/pallas_call | solution.py:27
  11.7 846.3 %shard_map.76 = (bf16[2,2,2048,1536]{3,2,1,0:T(8,128)(2,1)}, bf16[2,2,768,2048]{3,2,1,0:T(8,128)(2,1)}, bf16[2,4,2048,1536]{3,2,1,0:T(8,128)(2,1)}, bf16[2,4,768,2048]{3,2,1,0:T(8,128)(2,1)}) custom-call(s32[4]{0:T(128)S(1)} %get-tuple-element.11.owner_ref, bf16[1,8,2048,384]{3,2,1,0:T(8,128)(2,1)} %wg.1, bf16[1,8,2048,384]{3,2,1,0:T(8,128)(2,1)} %wu.1, ...), custom_call_target="tpu_custom_call" | custom-call | tf_op jit(solution)/shard_map/pallas_call | solution.py:288
  858.0 0.0 copy-start
  858.0 21.4 %copy.12 = bf16[2,2,2048,1536]{3,2,1,0:T(8,128)(2,1)} copy(bf16[2,2,2048,1536]{3,2,1,0:T(8,128)(2,1)} %get-tuple-element.16) | data formatting | bytes 50331648
  879.5 0.0 copy-done
  879.5 4.8 copy.13
  884.2 33.7 %copy.14 = bf16[2,4,2048,1536]{3,2,1,0:T(8,128)(2,1)} copy(bf16[2,4,2048,1536]{3,2,1,0:T(8,128)(2,1)} %get-tuple-element.18) | data formatting | bytes 100663296
  917.9 21.1 %copy.15 = bf16[2,4,768,2048]{3,2,1,0:T(8,128)(2,1)} copy(bf16[2,4,768,2048]{3,2,1,0:T(8,128)(2,1)} %get-tuple-element.19) | data formatting | bytes 50331648
Async XLA Ops:
  858.0 21.5 %copy-start = (bf16[2,2,768,2048]{3,2,1,0:T(8,128)(2,1)S(1)}, bf16[2,2,768,2048]{3,2,1,0:T(8,128)(2,1)}, u32[]{:S(2)}) copy-start(bf16[2,2,768,2048]{3,2,1,0:T(8,128)(2,1)} %get-tuple-element.17) | copy-start | bytes 37748740

commit v3 on v1

--- a/solution.py
+++ b/solution.py
@@ -45,8 +45,8 @@
 
 
 def move_kernel(
-    owner_ref, wg, wu, wd, pg, pu, pd, o13, o2, h13, h2,
-    own13, own2, par13, par2, far13, far2,
+    owner_ref, wg, wu, wd, pg, pu, pd, o13, o2, h13, h2, t0, t1, t2, t3,
+    own13, own2, par13, par2, far13, far2, held, t_sem,
     rg_send, rg_recv, loc_sem, dd_send, dd_recv, x_send, x_recv,
     n_send, n_recv, q_send, q_recv, w_sem,
 ):
@@ -86,7 +86,7 @@
         b1, b2 = (z + i) % 2, (c + j) % 2
         src = (wg, wu, wd)[w].at[0, 4 * b2 + 2 * b1 + b0]
         if w == 2:
-            dst = o2.at[y, b0, pl.ds(pl.multiple_of(z * f_loc, 128), f_loc)]
+            dst = o2.at[y, pl.ds(pl.multiple_of(z * f_loc, 128), f_loc)]
         else:
             dst = o13.at[y, b0, :, cols(z, w)]
         return src, dst, rg_recv.at[w, b0, y * 2 + z], (b1, x, c * 2 + b2)
@@ -118,7 +118,18 @@
         def _():
             home_copy(j, i, b0, w).wait_send()
 
-    homes = [(j, i, b0, w) for b0 in range(2) for w in range(3) for j in range(2) for i in range(2)]
+    homes = [
+        (j, i, b0, w)
+        for b0 in range(2) for w in range(3) for j in range(2) for i in range(2) if (b0, w) != (1, 2)
+    ]
+
+    tails = []
+    for n in range(4):
+        e = 4 * ((c + y + n % 2) % 2) + 2 * ((z + n // 2) % 2) + 1
+        tails.append((
+            pltpu.make_async_copy(wd.at[0, e], held.at[n], t_sem.at[0, n]),
+            pltpu.make_async_copy(held.at[n], (t0, t1, t2, t3)[n], t_sem.at[1, n]),
+        ))
 
     CH = range(6)
     dd = [remote(picked(2 * (1 - c) + k // 3, k % 3), vmem(par13, par2, k), dd_send.at[k], dd_recv.at[k], partner) for k in CH]
@@ -188,6 +199,11 @@
     def landed(at, sem):
         pltpu.make_async_copy(at, at, sem).wait()
 
+    for load, _ in tails:
+        load.start()
+    for load, store in tails:
+        load.wait()
+        store.start()
     for k in CH:
         xs[k].wait_recv()
         owner = owner_ref[2 * c + k // 3]
@@ -215,6 +231,8 @@
         landed(at, n_recv.at[2, k])
         pass_on.start()
 
+    for _, store in tails:
+        store.wait()
     for k in CH:
         dd[k].wait_send()
         to_y, to_z, to_p, to_self = fan(k)
@@ -235,14 +253,92 @@
     for b in homes:
         home_sent(*b)
     for w in range(3):
-        for b0 in range(2):
+        for b0 in range(1 if w == 2 else 2):
             for lay in range(2):
                 for half in range(2):
                     if w == 2:
-                        at = o2.at[lay, b0, pl.ds(half * f_loc, f_loc)]
+                        at = o2.at[lay, pl.ds(half * f_loc, f_loc)]
                     else:
                         at = o13.at[lay, b0, :, pl.ds(half * f_loc + w * f_all, f_loc)]
                     landed(at, rg_recv.at[w, b0, lay * 2 + half])
+
+
+def settle_kernel(o13, o2, h13, h2, q13, q2, g13, g2, buf13, buf2, sems):
+    slots = buf13.shape[0]
+    rows13, rows2 = buf13.shape[1], buf2.shape[1]
+
+    def tiles(src, dst, rows, buf):
+        return [
+            (src.at[pl.ds(r, rows)], dst.at[pl.ds(r, rows)], buf) for r in range(0, src.shape[0], rows)
+        ]
+
+    work = []
+    for lay in range(2):
+        for n in range(o13.shape[1]):
+            work += tiles(o13.at[lay, n], q13.at[lay, n], rows13, buf13)
+        work += tiles(o2.at[lay], q2.at[lay, 0], rows2, buf2)
+        for n in range(h13.shape[1]):
+            work += tiles(h13.at[lay, n], g13.at[lay, n], rows13, buf13)
+            work += tiles(h2.at[lay, n], g2.at[lay, n], rows2, buf2)
+
+    used = {id(buf13): 0, id(buf2): 0}
+    steps = []
+    last = {}
+    for src, dst, buf in work:
+        kind = 0 if buf is buf13 else 1
+        slot = used[id(buf)] % slots
+        used[id(buf)] += 1
+        before = last.get((kind, slot))
+        step = (
+            pltpu.make_async_copy(src, buf.at[slot], sems.at[kind, 0, slot]),
+            pltpu.make_async_copy(buf.at[slot], dst, sems.at[kind, 1, slot]),
+            before,
+        )
+        last[kind, slot] = step
+        steps.append(step)
+    lag = slots // 2
+    for n in range(len(steps) + lag):
+        if n < len(steps):
+            load, _, before = steps[n]
+            if before is not None:
+                before[1].wait()
+            load.start()
+        if n >= lag:
+            load, store, _ = steps[n - lag]
+            load.wait()
+            store.start()
+    for step in last.values():
+        step[1].wait()
+
+
+def place_kernel(t0, t1, r0, r1, r2, r3, q2_in, q2, buf, sems):
+    z = lax.axis_index("fs")
+    y = lax.axis_index("pp")
+    ep = lax.axis_index("ep")
+    x, c = ep // 2, ep % 2
+    f_loc = buf.shape[1]
+
+    def each(n, what):
+        source = (r0, r1, r2, r3)[n]
+        if n >= 2:
+            what(source)
+            return
+        here = (x == y) & (c == x) & (y == n)
+        pl.when(here)(lambda: what((t0, t1)[n]))
+        pl.when(jnp.logical_not(here))(lambda: what(source))
+
+    def store(n):
+        lay, half = (c + x + n % 2) % 2, (z + n // 2) % 2
+        rows = pl.ds(pl.multiple_of(half * f_loc, 128), f_loc)
+        return pltpu.make_async_copy(buf.at[n], q2.at[lay, 1, rows], sems.at[1, n])
+
+    for n in range(4):
+        each(n, lambda src: pltpu.make_async_copy(src, buf.at[n], sems.at[0, n]).start())
+    for n in range(4):
+        pltpu.make_async_copy(r0, buf.at[n], sems.at[0, n]).wait()
+        store(n).start()
+    for n in range(4):
+        store(n).wait()
 
 
 def solution(mesh):
@@ -250,6 +346,19 @@
     in_spec = P("pp", "ep", None, "fs")
     down_spec = P("pp", "ep", "fs", None)
     home_spec = P(None, ("pp", "ep", "fs"), None, None)
+
+    def tail_pairs(n):
+        pairs = []
+        for z in range(fs_size):
+            for y in range(pp_size):
+                for ep in range(ep_size):
+                    x, c = ep // 2, ep % 2
+                    b1, b2 = (z + n // 2) % 2, (c + y + n % 2) % 2
+                    src = (z * pp_size + y) * ep_size + ep
+                    dst = (b1 * pp_size + x) * ep_size + c * 2 + b2
+                    if src != dst:
+                        pairs.append((src, dst))
+        return pairs
 
     def device_body(w_gate, w_up, w_down, hot_ids):
         dtype = w_gate.dtype
@@ -263,23 +372,50 @@
         dma = pltpu.SemaphoreType.DMA
         buf13 = pltpu.VMEM((4, d_model, f_loc), dtype)
         buf2 = pltpu.VMEM((2, f_loc, d_model), dtype)
-        return pl.pallas_call(
+        shape = lambda *dims: jax.ShapeDtypeStruct(dims, dtype)
+        held = pltpu.VMEM((4, f_loc, d_model), dtype)
+        o13, o2, h13, h2, *tail = pl.pallas_call(
             move_kernel,
             out_shape=[
-                jax.ShapeDtypeStruct((layers, home, d_model, 2 * f_all), dtype),
-                jax.ShapeDtypeStruct((layers, home, f_all, d_model), dtype),
-                jax.ShapeDtypeStruct((layers, hot, d_model, 2 * f_all), dtype),
-                jax.ShapeDtypeStruct((layers, hot, f_all, d_model), dtype),
-            ],
+                shape(layers, home, d_model, 2 * f_all),
+                shape(layers, f_all, d_model),
+                shape(layers, hot, d_model, 2 * f_all),
+                shape(layers, hot, f_all, d_model),
+            ] + [shape(f_loc, d_model)] * 4,
             in_specs=[pl.BlockSpec(memory_space=pltpu.SMEM)] + [ANY] * 6,
-            out_specs=[ANY] * 4,
+            out_specs=[ANY] * 8,
             scratch_shapes=[
-                buf13, buf2, buf13, buf2, buf13, buf2,
+                buf13, buf2, buf13, buf2, buf13, buf2, held, dma((2, 4)),
                 dma((3, 8)), dma((3, 2, 4)), dma((6,)), dma((6,)), dma((6,)), dma((6,)), dma((6,)),
                 dma((3, 6)), dma((3, 6)), dma((4, 6)), dma((4, 6)), dma((6,)),
             ],
             compiler_params=pltpu.CompilerParams(has_side_effects=True, vmem_limit_bytes=48 * 1024 * 1024),
         )(owner, w_gate, w_up, w_down, *picked)
+        moved = [lax.ppermute(t, ("fs", "pp", "ep"), tail_pairs(n)) for n, t in enumerate(tail)]
+        copied = 4 * (o13.size + o2.size + h13.size + h2.size)
+        q13, q2, g13, g2 = pl.pallas_call(
+            settle_kernel,
+            out_shape=[
+                shape(*o13.shape), shape(layers, home, f_all, d_model), shape(*h13.shape), shape(*h2.shape),
+            ],
+            in_specs=[ANY] * 4,
+            out_specs=[ANY] * 4,
+            scratch_shapes=[
+                pltpu.VMEM((12, 512, 2 * f_all), dtype), pltpu.VMEM((12, f_loc, d_model), dtype), dma((2, 2, 12)),
+            ],
+            cost_estimate=pl.CostEstimate(flops=10**9, bytes_accessed=copied, transcendentals=0),
+            compiler_params=pltpu.CompilerParams(vmem_limit_bytes=48 * 1024 * 1024),
+        )(o13, o2, h13, h2)
+        q2 = pl.pallas_call(
+            place_kernel,
+            out_shape=shape(*q2.shape),
+            in_specs=[ANY] * 7,
+            out_specs=ANY,
+            scratch_shapes=[held, dma((2, 4))],
+            input_output_aliases={6: 0},
+            compiler_params=pltpu.CompilerParams(vmem_limit_bytes=56 * 1024 * 1024),
+        )(tail[0], tail[1], *moved, q2)
+        return q13, q2, g13, g2
 
     return jax.shard_map(
         device_body,

time: 880 us -> 845 us (0.960)
  local copies, waits for them, and re-layouts: 81 us -> 2.4 us
  waiting for transfers between devices: 0 us -> 25.5 us
  starting transfers between devices: 0 us -> 10 us
    unnamed x6 -> x12, local copies, waits for them, and re-layouts: 81 us -> 2.4 us
    ppermute x0 -> x4, waiting for transfers between devices: none -> 25.5 us  [device_body(): lax.ppermute(t, ('fs', 'pp', 'ep'), tail_pairs(n))]
    ppermute x0 -> x4, starting transfers between devices: none -> 10 us  [device_body(): lax.ppermute(t, ('fs', 'pp', 'ep'), tail_pairs(n))]
    pallas_call x1 -> x3, Pallas kernels: 783 us -> 790 us  [the longest x1 717 us: device_body(): pl.pallas_call(move_kernel, out_shape=[shape(layers, home, d_model, 2 * f...]
  transfers between devices with their start and end apart: 0 -> 4, of which waited for: 0 -> 1; matrix products, arithmetic and copies ran while one was open for 0% -> 0% of each run, Pallas kernels for 0% -> 8%
where the time goes in v3:
time: 845 us; the launch traced here: 843 us
  Pallas kernels  803 us (95%)
  waiting for transfers between devices  25.5 us (3%)
  starting transfers between devices  10 us (1%)
    pallas_call x1, Pallas kernels, device_body(): pl.pallas_call(move_kernel, out_shape=[shape(layers, home, d_model, 2 * f...  717 us
    pallas_call x1, Pallas kernels, device_body(): pl.pallas_call(settle_kernel, out_shape=[shape(*o13.shape), shape(layers,...  68.3 us
    ppermute x4, waiting for transfers between devices, device_body(): lax.ppermute(t, ('fs', 'pp', 'ep'), tail_pairs(n))  25.5 us
  transfers between devices with their start and end apart: 4, of which 1 were waited for; matrix products, arithmetic and copies ran while one was open for 0% of the time, Pallas kernels for 8%

profile of v3, /device:TPU:2, one launch (start us, length us, event | category | flops | bytes accessed | tf_op | source)
XLA Modules:
  0.0 843.2 jit_solution(14129014556751590048)
XLA Ops:
  0.6 1.2 subtract_clamp_fusion
  1.8 13.3 %shard_map.75 = (bf16[4,2048,384]{2,1,0:T(8,128)(2,1)}, bf16[4,2048,384]{2,1,0:T(8,128)(2,1)}, bf16[4,384,2048]{2,1,0:T(8,128)(2,1)}) custom-call(s32[4]{0:T(128)} %get-tuple-element.34.off_ref, bf16[1,8,2048,384]{3,2,1,0:T(8,128)(2,1)} %wg.1, bf16[1,8,2048,384]{3,2,1,0:T(8,128)(2,1)} %wu.1, bf16[1,8,384,2048]{3,2,1,0:T(8,128)(2,1)} %wd.1), custom_call_target="tpu_custom_call" | custom-call | tf_op jit(solution)/shard_map/pallas_call | solution.py:27
  15.1 716.6 %shard_map.76 = (bf16[2,2,2048,1536]{3,2,1,0:T(8,128)(2,1)}, bf16[2,768,2048]{2,1,0:T(8,128)(2,1)}, bf16[2,4,2048,1536]{3,2,1,0:T(8,128)(2,1)}, bf16[2,4,768,204...) custom-call(s32[4]{0:T(128)S(1)} %get-tuple-element.35.owner_ref, ...), custom_call_target="tpu_custom_call" | custom-call | tf_op jit(solution)/shard_map/pallas_call | solution.py:377
  731.7 0.0 copy-start
  731.7 0.0 copy-start.1
  731.7 3.0 collective-permute-start
  734.8 3.4 collective-permute-start.1
  738.2 0.1 collective-permute-start.2
  738.3 3.5 collective-permute-start.3
  741.8 68.3 %shard_map.77 = (bf16[2,2,2048,1536]{3,2,1,0:T(8,128)(2,1)}, bf16[2,2,768,2048]{3,2,1,0:T(8,128)(2,1)}, bf16[2,4,2048,1536]{3,2,1,0:T(8,128)(2,1)}, bf16[2,4,768,2048]{3,2,1,0:T(8,128)(2,1)}) custom-call(bf16[2,2,2048,1536]{3,2,1,0:T(8,128)(2,1)} %get-tuple-element.22.o13, bf16[2,768,2048]{2,1,0:T(8,128)(2,1)} %get-tuple-element.23.o2, ...), custom_call_target="tpu_custom_call" | custom-call | flops 1000000000 | bytes 213909504 | tf_op jit(solution)/shard_map/pallas_call | solution.py:396
  810.1 0.0 copy-done
  810.1 0.0 copy-done.1
  810.1 0.0 collective-permute-done.r0
  810.1 0.0 copy-start.2
  810.1 0.0 collective-permute-done.1.r1
  810.1 0.0 copy-start.3
  810.1 0.0 collective-permute-done.2.r2
  810.1 0.0 copy-start.4
  810.2 1.2 copy-done.4
  811.4 25.5 %collective-permute-done.3.r3 = bf16[384,2048]{1,0:T(8,128)(2,1)S(1)} collective-permute-done((bf16[384,2048]{1,0:T(8,128)(2,1)}, bf16[384,2048]{1,0:T(8,128)(2,1)S(1)}, u32[]{:S(2)}, u32[]{:S(2)}) %collective-permute-start.3) | collective-permute-done | bytes 1572896 | tf_op jit(solution)/shard_map/ppermute | solution.py:394
  836.9 0.0 copy-start.5
  836.9 1.2 copy-done.5
  838.0 0.0 copy-done.2
  838.0 0.0 copy-done.3
  838.0 5.2 shard_map.78
Async XLA Ops:
  731.7 78.4 %copy-start = (bf16[384,2048]{1,0:T(8,128)(2,1)}, bf16[384,2048]{1,0:T(8,128)(2,1)S(1)}, u32[]{:S(2)}) copy-start(bf16[384,2048]{1,0:T(8,128)(2,1)S(1)} %get-tuple-element.27.t0) | copy-start | bytes 4718596
  731.7 78.4 %copy-start.1 = (bf16[384,2048]{1,0:T(8,128)(2,1)}, bf16[384,2048]{1,0:T(8,128)(2,1)S(1)}, u32[]{:S(2)}) copy-start(bf16[384,2048]{1,0:T(8,128)(2,1)S(1)} %get-tuple-element.28.t1) | copy-start | bytes 4718596
  731.7 78.4 %collective-permute-start = (bf16[384,2048]{1,0:T(8,128)(2,1)S(1)}, bf16[384,2048]{1,0:T(8,128)(2,1)S(1)}, u32[]{:S(2)}, u32[]{:S(2)}) collective-permute-start(bf16[384,2048]{1,0:T(8,128)(2,1)S(1)} %get-tuple-element.27.t0), channel_id=1, source_target_pairs={{1,3},{2,4},{3,7},{4,1},{5,2},{6,5},{7,6},{9,11},{10,12},{11,15},{... | collective-permute-start | bytes 4718600 | tf_op jit(solution)/shard_map/ppermute | solution.py:394
  734.8 75.3 %collective-permute-start.1 = (bf16[384,2048]{1,0:T(8,128)(2,1)S(1)}, bf16[384,2048]{1,0:T(8,128)(2,1)S(1)}, u32[]{:S(2)}, u32[]{:S(2)}) collective-permute-start(bf16[384,2048]{1,0:T(8,128)(2,1)S(1)} %get-tuple-element.28.t1), channel_id=1, source_target_pairs={{0,1},{1,2},{2,5},{3,6},{4,0},{5,3},{6,4},{8,9},{9,10},{10,13},{11... | collective-permute-start | bytes 4718600 | tf_op jit(solution)/shard_map/ppermute | solution.py:394
  738.2 71.9 %collective-permute-start.2 = (bf16[384,2048]{1,0:T(8,128)(2,1)S(1)}, bf16[384,2048]{1,0:T(8,128)(2,1)S(1)}, u32[]{:S(2)}, u32[]{:S(2)}) collective-permute-start(bf16[384,2048]{1,0:T(8,128)(2,1)S(1)} %get-tuple-element.29), channel_id=1, source_target_pairs={{0,8},{1,11},{2,12},{3,15},{4,9},{5,10},{6,13},{7,14},{8,0},{9,3},... | collective-permute-start | bytes 4718600 | tf_op jit(solution)/shard_map/ppermute | solution.py:394
  738.3 98.6 %collective-permute-start.3 = (bf16[384,2048]{1,0:T(8,128)(2,1)}, bf16[384,2048]{1,0:T(8,128)(2,1)S(1)}, u32[]{:S(2)}, u32[]{:S(2)}) collective-permute-start(bf16[384,2048]{1,0:T(8,128)(2,1)} %get-tuple-element.30), channel_id=1, source_target_pairs={{0,9},{1,10},{2,13},{3,14},{4,8},{5,11},{6,12},{7,15},{8,1},{9,2},... | collective-permute-start | bytes 4718600 | tf_op jit(solution)/shard_map/ppermute | solution.py:394
  810.1 27.9 %copy-start.2 = (bf16[384,2048]{1,0:T(8,128)(2,1)}, bf16[384,2048]{1,0:T(8,128)(2,1)S(1)}, u32[]{:S(2)}) copy-start(bf16[384,2048]{1,0:T(8,128)(2,1)S(1)} %collective-permute-done.r0) | copy-start | bytes 4718596
  810.1 27.9 %copy-start.3 = (bf16[384,2048]{1,0:T(8,128)(2,1)}, bf16[384,2048]{1,0:T(8,128)(2,1)S(1)}, u32[]{:S(2)}) copy-start(bf16[384,2048]{1,0:T(8,128)(2,1)S(1)} %collective-permute-done.1.r1) | copy-start | bytes 4718596
  810.1 1.2 copy-start.4
  836.9 1.2 copy-start.5

commit v4 on v3

--- a/solution.py
+++ b/solution.py
@@ -45,10 +45,10 @@
 
 
 def move_kernel(
-    owner_ref, wg, wu, wd, pg, pu, pd, o13, o2, h13, h2, t0, t1, t2, t3,
+    owner_ref, wg, wu, wd, pg, pu, pd, o13, o2, o2b, h13, h2, t0, t1, t2, t3,
     own13, own2, par13, par2, far13, far2, held, t_sem,
     rg_send, rg_recv, loc_sem, dd_send, dd_recv, x_send, x_recv,
-    n_send, n_recv, q_send, q_recv, w_sem,
+    n_send, n_recv, f_send, q_send, q_recv, w_sem,
 ):
     z = lax.axis_index("fs")
     y = lax.axis_index("pp")
@@ -56,6 +56,8 @@
     x, c = ep // 2, ep % 2
     d_model, f_loc = wg.shape[2], wg.shape[3]
     f_all = f_loc * 2
+    tail_rows = t0.shape[0]
+    kept = f_loc - tail_rows
     partner = (z, y, x * 2 + 1 - c)
     x_nbr = (z, y, (1 - x) * 2 + c)
     y_nbr = (z, 1 - y, ep)
@@ -85,7 +87,10 @@
     def home_refs(j, i, b0, w):
         b1, b2 = (z + i) % 2, (c + j) % 2
         src = (wg, wu, wd)[w].at[0, 4 * b2 + 2 * b1 + b0]
-        if w == 2:
+        if w == 2 and b0 == 1:
+            src = src.at[pl.ds(tail_rows, kept)]
+            dst = o2b.at[y, pl.ds(pl.multiple_of(z * kept, 128), kept)]
+        elif w == 2:
             dst = o2.at[y, pl.ds(pl.multiple_of(z * f_loc, 128), f_loc)]
         else:
             dst = o13.at[y, b0, :, cols(z, w)]
@@ -120,14 +125,14 @@
 
     homes = [
         (j, i, b0, w)
-        for b0 in range(2) for w in range(3) for j in range(2) for i in range(2) if (b0, w) != (1, 2)
+        for b0 in range(2) for w in range(3) for j in range(2) for i in range(2)
     ]
 
     tails = []
     for n in range(4):
         e = 4 * ((c + y + n % 2) % 2) + 2 * ((z + n // 2) % 2) + 1
         tails.append((
-            pltpu.make_async_copy(wd.at[0, e], held.at[n], t_sem.at[0, n]),
+            pltpu.make_async_copy(wd.at[0, e, pl.ds(0, tail_rows)], held.at[n], t_sem.at[0, n]),
             pltpu.make_async_copy(held.at[n], (t0, t1, t2, t3)[n], t_sem.at[1, n]),
         ))
 
@@ -161,8 +166,19 @@
     for b in homes[2:4]:
         home_start(*b)
     xs[5].start()
-    for b in homes[4:]:
-        home_start(*b)
+
+    @pl.when(c != x)
+    def _():
+        for b in homes[4:]:
+            home_start(*b)
+
+    def spread(first, stop):
+        @pl.when(c == x)
+        def _():
+            for b in homes[first:stop]:
+                home_start(*b)
+
+    spread(4, 6)
 
     def hot_of(k):
         return 2 * c + k // 3
@@ -192,6 +208,16 @@
         at = hot_at(hot_of(k), y, 1 - z, k % 3)
         return remote(at, at, n_send.at[2, k], n_recv.at[2, k], y_nbr)
 
+    def across(k):
+        at = hot_at(hot_of(k), 1 - y, 1 - z, k % 3)
+        return remote(at, at, f_send.at[k], n_recv.at[2, k], x_nbr)
+
+    def onward_do(k, what):
+        if k < 4:
+            pl.when(c == x)(lambda: what(onward(k)))
+        else:
+            what(onward(k))
+
     def from_diag(k):
         at = hot_at(hot_of(k), 1 - y, 1 - z, k % 3)
         return at, remote(at, at, q_send.at[3, k], q_recv.at[3, k], partner)
@@ -211,24 +237,26 @@
         if k > 0:
             for copy in fan(k - 1):
                 copy.start()
-    for k in CH:
-        xs[k].wait_send()
+        spread(6 + k, 7 + k)
     for copy in fan(5):
         copy.start()
+    spread(12, len(homes))
     for k in CH:
         at, pass_on = from_y(k)
         landed(at, n_recv.at[0, k])
         if k % 2 == 0:
-            onward(k).start()
+            onward_do(k, lambda copy: copy.start())
         pass_on.start()
         at, pass_on = from_z(k)
         landed(at, n_recv.at[1, k])
         if k % 2 == 1:
-            onward(k).start()
+            onward_do(k, lambda copy: copy.start())
         pass_on.start()
     for k in CH:
         at, pass_on = from_diag(k)
         landed(at, n_recv.at[2, k])
+        if k < 4:
+            pl.when(c == x)(lambda: across(k).start())
         pass_on.start()
 
     for _, store in tails:
@@ -240,7 +268,10 @@
         to_z.wait_send()
         to_p.wait_send()
         to_self.wait()
-        onward(k).wait_send()
+        xs[k].wait_send()
+        onward_do(k, lambda copy: copy.wait_send())
+        if k < 4:
+            pl.when(c == x)(lambda: across(k).wait_send())
         from_y(k)[1].wait_send()
         from_z(k)[1].wait_send()
         from_diag(k)[1].wait_send()
@@ -253,17 +284,19 @@
     for b in homes:
         home_sent(*b)
     for w in range(3):
-        for b0 in range(1 if w == 2 else 2):
+        for b0 in range(2):
             for lay in range(2):
                 for half in range(2):
-                    if w == 2:
+                    if w == 2 and b0 == 1:
+                        at = o2b.at[lay, pl.ds(half * kept, kept)]
+                    elif w == 2:
                         at = o2.at[lay, pl.ds(half * f_loc, f_loc)]
                     else:
                         at = o13.at[lay, b0, :, pl.ds(half * f_loc + w * f_all, f_loc)]
                     landed(at, rg_recv.at[w, b0, lay * 2 + half])
 
 
-def settle_kernel(o13, o2, h13, h2, q13, q2, g13, g2, buf13, buf2, sems):
+def settle_kernel(o13, o2, o2b, h13, h2, q13, q2, g13, g2, buf13, buf2, sems):
     slots = buf13.shape[0]
     rows13, rows2 = buf13.shape[1], buf2.shape[1]
 
@@ -271,12 +304,17 @@
         return [
             (src.at[pl.ds(r, rows)], dst.at[pl.ds(r, rows)], buf) for r in range(0, src.shape[0], rows)
         ]
+
+    kept = o2b.shape[1] // 2
 
     work = []
     for lay in range(2):
         for n in range(o13.shape[1]):
             work += tiles(o13.at[lay, n], q13.at[lay, n], rows13, buf13)
         work += tiles(o2.at[lay], q2.at[lay, 0], rows2, buf2)
+        for half in range(2):
+            put = q2.at[lay, 1, pl.ds((half + 1) * rows2 - kept, kept)]
+            work.append((o2b.at[lay, pl.ds(half * kept, kept)], put, buf2))
         for n in range(h13.shape[1]):
             work += tiles(h13.at[lay, n], g13.at[lay, n], rows13, buf13)
             work += tiles(h2.at[lay, n], g2.at[lay, n], rows2, buf2)
@@ -289,9 +327,10 @@
         slot = used[id(buf)] % slots
         used[id(buf)] += 1
         before = last.get((kind, slot))
+        tile = buf.at[slot, pl.ds(0, src.shape[0])]
         step = (
-            pltpu.make_async_copy(src, buf.at[slot], sems.at[kind, 0, slot]),
-            pltpu.make_async_copy(buf.at[slot], dst, sems.at[kind, 1, slot]),
+            pltpu.make_async_copy(src, tile, sems.at[kind, 0, slot]),
+            pltpu.make_async_copy(tile, dst, sems.at[kind, 1, slot]),
             before,
         )
         last[kind, slot] = step
@@ -316,7 +355,7 @@
     y = lax.axis_index("pp")
     ep = lax.axis_index("ep")
     x, c = ep // 2, ep % 2
-    f_loc = buf.shape[1]
+    f_loc, tail_rows = q2.shape[2] // 2, buf.shape[1]
 
     def each(n, what):
         source = (r0, r1, r2, r3)[n]
@@ -329,7 +368,7 @@
 
     def store(n):
         lay, half = (c + x + n % 2) % 2, (z + n // 2) % 2
-        rows = pl.ds(pl.multiple_of(half * f_loc, 128), f_loc)
+        rows = pl.ds(pl.multiple_of(half * f_loc, 128), tail_rows)
         return pltpu.make_async_copy(buf.at[n], q2.at[lay, 1, rows], sems.at[1, n])
 
     for n in range(4):
@@ -373,21 +412,23 @@
         buf13 = pltpu.VMEM((4, d_model, f_loc), dtype)
         buf2 = pltpu.VMEM((2, f_loc, d_model), dtype)
         shape = lambda *dims: jax.ShapeDtypeStruct(dims, dtype)
-        held = pltpu.VMEM((4, f_loc, d_model), dtype)
-        o13, o2, h13, h2, *tail = pl.pallas_call(
+        tail_rows = f_loc * 2 // 3
+        held = pltpu.VMEM((4, tail_rows, d_model), dtype)
+        o13, o2, o2b, h13, h2, *tail = pl.pallas_call(
             move_kernel,
             out_shape=[
                 shape(layers, home, d_model, 2 * f_all),
                 shape(layers, f_all, d_model),
+                shape(layers, f_all - fs_size * tail_rows, d_model),
                 shape(layers, hot, d_model, 2 * f_all),
                 shape(layers, hot, f_all, d_model),
-            ] + [shape(f_loc, d_model)] * 4,
+            ] + [shape(tail_rows, d_model)] * 4,
             in_specs=[pl.BlockSpec(memory_space=pltpu.SMEM)] + [ANY] * 6,
-            out_specs=[ANY] * 8,
+            out_specs=[ANY] * 9,
             scratch_shapes=[
                 buf13, buf2, buf13, buf2, buf13, buf2, held, dma((2, 4)),
                 dma((3, 8)), dma((3, 2, 4)), dma((6,)), dma((6,)), dma((6,)), dma((6,)), dma((6,)),
-                dma((3, 6)), dma((3, 6)), dma((4, 6)), dma((4, 6)), dma((6,)),
+                dma((3, 6)), dma((3, 6)), dma((4,)), dma((4, 6)), dma((4, 6)), dma((6,)),
             ],
             compiler_params=pltpu.CompilerParams(has_side_effects=True, vmem_limit_bytes=48 * 1024 * 1024),
         )(owner, w_gate, w_up, w_down, *picked)
@@ -398,14 +439,14 @@
             out_shape=[
                 shape(*o13.shape), shape(layers, home, f_all, d_model), shape(*h13.shape), shape(*h2.shape),
             ],
-            in_specs=[ANY] * 4,
+            in_specs=[ANY] * 5,
             out_specs=[ANY] * 4,
             scratch_shapes=[
                 pltpu.VMEM((12, 512, 2 * f_all), dtype), pltpu.VMEM((12, f_loc, d_model), dtype), dma((2, 2, 12)),
             ],
             cost_estimate=pl.CostEstimate(flops=10**9, bytes_accessed=copied, transcendentals=0),
             compiler_params=pltpu.CompilerParams(vmem_limit_bytes=48 * 1024 * 1024),
-        )(o13, o2, h13, h2)
+        )(o13, o2, o2b, h13, h2)
         q2 = pl.pallas_call(
             place_kernel,
             out_shape=shape(*q2.shape),

time: 845 us -> 850 us (level)
  waiting for transfers between devices: 25.5 us -> 0.01 us
  Pallas kernels: 803 us -> 827 us
    ppermute x4, waiting for transfers between devices: 25.5 us -> 0.01 us  [device_body(): lax.ppermute(t, ('fs', 'pp', 'ep'), tail_pairs(n))]
    pallas_call x1, Pallas kernels: 717 us -> 741 us  [device_body(): pl.pallas_call(move_kernel, out_shape=[shape(layers, home, d_model, 2 * f...]
  transfers between devices with their start and end apart: 4 -> 4, of which waited for: 1 -> 0; matrix products, arithmetic and copies ran while one was open for 0% -> 0% of each run, Pallas kernels for 8% -> 8%
where the time goes in v4:
time: 850 us; the launch traced here: 848 us
  Pallas kernels  827 us (97%)
  starting transfers between devices  15.5 us (2%)
    pallas_call x1, Pallas kernels, device_body(): pl.pallas_call(move_kernel, out_shape=[shape(layers, home, d_model, 2 * f...  741 us
    pallas_call x1, Pallas kernels, device_body(): pl.pallas_call(settle_kernel, out_shape=[shape(*o13.shape), shape(layers,...  69.6 us
  transfers between devices with their start and end apart: 4, of which 0 were waited for; matrix products, arithmetic and copies ran while one was open for 0% of the time, Pallas kernels for 8%

profile of v4, /device:TPU:2, one launch (start us, length us, event | category | flops | bytes accessed | tf_op | source)
XLA Modules:
  0.0 848.4 jit_solution(17015589339969976805)
XLA Ops:
  0.6 1.2 subtract_clamp_fusion
  1.8 13.1 %shard_map.75 = (bf16[4,2048,384]{2,1,0:T(8,128)(2,1)}, bf16[4,2048,384]{2,1,0:T(8,128)(2,1)}, bf16[4,384,2048]{2,1,0:T(8,128)(2,1)}) custom-call(s32[4]{0:T(128)} %get-tuple-element.36.off_ref, bf16[1,8,2048,384]{3,2,1,0:T(8,128)(2,1)} %wg.1, bf16[1,8,2048,384]{3,2,1,0:T(8,128)(2,1)} %wu.1, bf16[1,8,384,2048]{3,2,1,0:T(8,128)(2,1)} %wd.1), custom_call_target="tpu_custom_call" | custom-call | tf_op jit(solution)/shard_map/pallas_call | solution.py:27
  14.9 741.5 %shard_map.76 = (bf16[2,2,2048,1536]{3,2,1,0:T(8,128)(2,1)}, bf16[2,768,2048]{2,1,0:T(8,128)(2,1)}, bf16[2,256,2048]{2,1,0:T(8,128)(2,1)}, bf16[2,4,2048,1536]{3...) custom-call(s32[4]{0:T(128)S(1)} %get-tuple-element.37.owner_ref, ...), custom_call_target="tpu_custom_call" | custom-call | tf_op jit(solution)/shard_map/pallas_call | solution.py:417
  756.4 0.0 copy-start.1
  756.4 0.0 copy-start.2
  756.4 10.0 %collective-permute-start = (bf16[256,2048]{1,0:T(8,128)(2,1)S(1)}, bf16[256,2048]{1,0:T(8,128)(2,1)S(1)}, u32[]{:S(2)}, u32[]{:S(2)}) collective-permute-start(bf16[256,2048]{1,0:T(8,128)(2,1)S(1)} %get-tuple-element.29.t0), channel_id=1, source_target_pairs={{1,3},{2,4},{3,7},{4,1},{5,2},{6,5},{7,6},{9,11},{10,12},{11,15},{... | collective-permute-start | bytes 3145736 | tf_op jit(solution)/shard_map/ppermute | solution.py:435
  766.4 1.9 collective-permute-start.1
  768.3 0.2 collective-permute-start.2
  768.5 3.4 collective-permute-start.3
  771.9 0.0 copy-start
  771.9 1.6 copy-done
  773.5 69.6 %shard_map.77 = (bf16[2,2,2048,1536]{3,2,1,0:T(8,128)(2,1)}, bf16[2,2,768,2048]{3,2,1,0:T(8,128)(2,1)}, bf16[2,4,2048,1536]{3,2,1,0:T(8,128)(2,1)}, bf16[2,4,768,2048]{3,2,1,0:T(8,128)(2,1)}) custom-call(bf16[2,2,2048,1536]{3,2,1,0:T(8,128)(2,1)} %get-tuple-element.23.o13, bf16[2,768,2048]{2,1,0:T(8,128)(2,1)} %get-tuple-element.24.o2, ...), custom_call_target="tpu_custom_call" | custom-call | flops 1000000000 | bytes 213909504 | tf_op jit(solution)/shard_map/pallas_call | solution.py:437
  843.1 0.0 copy-done.1
  843.1 0.0 copy-done.2
  843.1 0.0 collective-permute-done.r0
  843.1 0.0 copy-start.3
  843.2 0.0 collective-permute-done.1.r1
  843.2 0.0 copy-start.4
  843.2 0.0 collective-permute-done.2.r2
  843.2 0.0 copy-start.5
  843.2 0.0 collective-permute-done.3.r3
  843.2 0.0 copy-start.6
  843.2 1.0 copy-done.6
  844.3 0.2 copy-done.3
  844.5 0.4 copy-done.4
  844.8 0.3 copy-done.5
  845.1 3.3 shard_map.78
Async XLA Ops:
  756.4 86.8 %copy-start.1 = (bf16[256,2048]{1,0:T(8,128)(2,1)}, bf16[256,2048]{1,0:T(8,128)(2,1)S(1)}, u32[]{:S(2)}) copy-start(bf16[256,2048]{1,0:T(8,128)(2,1)S(1)} %get-tuple-element.29.t0) | copy-start | bytes 3145732
  756.4 86.8 %copy-start.2 = (bf16[256,2048]{1,0:T(8,128)(2,1)}, bf16[256,2048]{1,0:T(8,128)(2,1)S(1)}, u32[]{:S(2)}) copy-start(bf16[256,2048]{1,0:T(8,128)(2,1)S(1)} %get-tuple-element.30.t1) | copy-start | bytes 3145732
  756.4 86.8 %collective-permute-start = (bf16[256,2048]{1,0:T(8,128)(2,1)S(1)}, bf16[256,2048]{1,0:T(8,128)(2,1)S(1)}, u32[]{:S(2)}, u32[]{:S(2)}) collective-permute-start(bf16[256,2048]{1,0:T(8,128)(2,1)S(1)} %get-tuple-element.29.t0), channel_id=1, source_target_pairs={{1,3},{2,4},{3,7},{4,1},{5,2},{6,5},{7,6},{9,11},{10,12},{11,15},{... | collective-permute-start | bytes 3145736 | tf_op jit(solution)/shard_map/ppermute | solution.py:435
  766.4 76.8 %collective-permute-start.1 = (bf16[256,2048]{1,0:T(8,128)(2,1)S(1)}, bf16[256,2048]{1,0:T(8,128)(2,1)S(1)}, u32[]{:S(2)}, u32[]{:S(2)}) collective-permute-start(bf16[256,2048]{1,0:T(8,128)(2,1)S(1)} %get-tuple-element.30.t1), channel_id=1, source_target_pairs={{0,1},{1,2},{2,5},{3,6},{4,0},{5,3},{6,4},{8,9},{9,10},{10,13},{11... | collective-permute-start | bytes 3145736 | tf_op jit(solution)/shard_map/ppermute | solution.py:435
  768.3 74.9 %collective-permute-start.2 = (bf16[256,2048]{1,0:T(8,128)(2,1)S(1)}, bf16[256,2048]{1,0:T(8,128)(2,1)S(1)}, u32[]{:S(2)}, u32[]{:S(2)}) collective-permute-start(bf16[256,2048]{1,0:T(8,128)(2,1)S(1)} %get-tuple-element.31), channel_id=1, source_target_pairs={{0,8},{1,11},{2,12},{3,15},{4,9},{5,10},{6,13},{7,14},{8,0},{9,3},... | collective-permute-start | bytes 3145736 | tf_op jit(solution)/shard_map/ppermute | solution.py:435
  768.5 74.7 %collective-permute-start.3 = (bf16[256,2048]{1,0:T(8,128)(2,1)S(1)}, bf16[256,2048]{1,0:T(8,128)(2,1)S(1)}, u32[]{:S(2)}, u32[]{:S(2)}) collective-permute-start(bf16[256,2048]{1,0:T(8,128)(2,1)S(1)} %get-tuple-element.32), channel_id=1, source_target_pairs={{0,9},{1,10},{2,13},{3,14},{4,8},{5,11},{6,12},{7,15},{8,1},{9,2},... | collective-permute-start | bytes 3145736 | tf_op jit(solution)/shard_map/ppermute | solution.py:435
  771.9 1.6 copy-start
  843.1 1.3 copy-start.3
  843.2 1.7 copy-start.4
  843.2 1.9 copy-start.5
  843.2 1.0 copy-start.6

commit v5 on v4

--- a/solution.py
+++ b/solution.py
@@ -44,43 +44,29 @@
     )(offset, w_gate, w_up, w_down)
 
 
-def move_kernel(
-    owner_ref, wg, wu, wd, pg, pu, pd, o13, o2, o2b, h13, h2, t0, t1, t2, t3,
-    own13, own2, par13, par2, far13, far2, held, t_sem,
-    rg_send, rg_recv, loc_sem, dd_send, dd_recv, x_send, x_recv,
-    n_send, n_recv, f_send, q_send, q_recv, w_sem,
-):
+def place_of_device():
     z = lax.axis_index("fs")
     y = lax.axis_index("pp")
     ep = lax.axis_index("ep")
-    x, c = ep // 2, ep % 2
-    d_model, f_loc = wg.shape[2], wg.shape[3]
+    return ep // 2, y, z, ep % 2
+
+
+def remote(src, dst, send, recv, dev):
+    return pltpu.make_async_remote_copy(
+        src_ref=src, dst_ref=dst, send_sem=send, recv_sem=recv, device_id=dev, device_id_type=MESH
+    )
+
+
+def landed(at, sem):
+    pltpu.make_async_copy(at, at, sem).wait()
+
+
+def home_kernel(wg, wu, wd, o13, o2, o2b, t0, t1, t2, t3, held, t_sem, rg_send, rg_recv):
+    x, y, z, c = place_of_device()
+    f_loc = wg.shape[3]
     f_all = f_loc * 2
     tail_rows = t0.shape[0]
     kept = f_loc - tail_rows
-    partner = (z, y, x * 2 + 1 - c)
-    x_nbr = (z, y, (1 - x) * 2 + c)
-    y_nbr = (z, 1 - y, ep)
-    z_nbr = (1 - z, y, ep)
-
-    def cols(half, up):
-        return pl.ds(pl.multiple_of(half * f_loc + up * f_all, 128), f_loc)
-
-    def remote(src, dst, send, recv, dev):
-        return pltpu.make_async_remote_copy(
-            src_ref=src, dst_ref=dst, send_sem=send, recv_sem=recv, device_id=dev, device_id_type=MESH
-        )
-
-    def vmem(b13, b2, k):
-        return b2.at[k // 3] if k % 3 == 2 else b13.at[(k // 3) * 2 + k % 3]
-
-    def picked(h, w):
-        return (pg, pu, pd)[w].at[h]
-
-    def hot_at(h, lay, half, w):
-        if w == 2:
-            return h2.at[lay, h, pl.ds(pl.multiple_of(half * f_loc, 128), f_loc)]
-        return h13.at[lay, h, :, cols(half, w)]
 
     stays = (x == y) & (c == x)
 
@@ -93,7 +79,7 @@
         elif w == 2:
             dst = o2.at[y, pl.ds(pl.multiple_of(z * f_loc, 128), f_loc)]
         else:
-            dst = o13.at[y, b0, :, cols(z, w)]
+            dst = o13.at[y, b0, :, pl.ds(pl.multiple_of(z * f_loc + w * f_all, 128), f_loc)]
         return src, dst, rg_recv.at[w, b0, y * 2 + z], (b1, x, c * 2 + b2)
 
     def home_copy(j, i, b0, w):
@@ -123,10 +109,7 @@
         def _():
             home_copy(j, i, b0, w).wait_send()
 
-    homes = [
-        (j, i, b0, w)
-        for b0 in range(2) for w in range(3) for j in range(2) for i in range(2)
-    ]
+    homes = [(j, i, b0, w) for b0 in range(2) for w in range(3) for j in range(2) for i in range(2)]
 
     tails = []
     for n in range(4):
@@ -136,151 +119,15 @@
             pltpu.make_async_copy(held.at[n], (t0, t1, t2, t3)[n], t_sem.at[1, n]),
         ))
 
-    CH = range(6)
-    dd = [remote(picked(2 * (1 - c) + k // 3, k % 3), vmem(par13, par2, k), dd_send.at[k], dd_recv.at[k], partner) for k in CH]
-    own = [pltpu.make_async_copy(picked(2 * c + k // 3, k % 3), vmem(own13, own2, k), loc_sem.at[k]) for k in CH]
-    xs = [remote(vmem(own13, own2, k), vmem(far13, far2, k), x_send.at[k], x_recv.at[k], x_nbr) for k in CH]
-
-    def choose(take_a, a, b, out):
-        rows = a.shape[0] // 8
-
-        def body(i, carry):
-            at = pl.ds(pl.multiple_of(i * rows, 16), rows)
-            out[at, :] = jnp.where(take_a, a[at, :], b[at, :])
-            return carry
-
-        lax.fori_loop(0, 8, body, 0)
-
-    for k in CH:
-        own[k].start()
-        dd[k].start()
-    for b in homes[:2]:
+    for b in homes:
         home_start(*b)
-    for k in CH:
-        own[k].wait()
-        dd[k].wait_recv()
-        owner = owner_ref[2 * c + k // 3]
-        choose(owner % 2 == c, vmem(own13, own2, k), vmem(par13, par2, k), vmem(own13, own2, k))
-        if k > 0:
-            xs[k - 1].start()
-    for b in homes[2:4]:
-        home_start(*b)
-    xs[5].start()
-
-    @pl.when(c != x)
-    def _():
-        for b in homes[4:]:
-            home_start(*b)
-
-    def spread(first, stop):
-        @pl.when(c == x)
-        def _():
-            for b in homes[first:stop]:
-                home_start(*b)
-
-    spread(4, 6)
-
-    def hot_of(k):
-        return 2 * c + k // 3
-
-    def fan(k):
-        src, w = vmem(par13, par2, k), k % 3
-        dst = hot_at(hot_of(k), y, z, w)
-        return (
-            remote(src, dst, n_send.at[0, k], n_recv.at[0, k], y_nbr),
-            remote(src, dst, n_send.at[1, k], n_recv.at[1, k], z_nbr),
-            remote(src, dst, q_send.at[0, k], q_recv.at[0, k], partner),
-            pltpu.make_async_copy(src, dst, w_sem.at[k]),
-        )
-
-    def from_y(k):
-        at = hot_at(hot_of(k), 1 - y, z, k % 3)
-        return at, remote(at, at, q_send.at[1, k], q_recv.at[1, k], partner)
-
-    def from_z(k):
-        at = hot_at(hot_of(k), y, 1 - z, k % 3)
-        return at, remote(at, at, q_send.at[2, k], q_recv.at[2, k], partner)
-
-    def onward(k):
-        if k % 2 == 0:
-            at = hot_at(hot_of(k), 1 - y, z, k % 3)
-            return remote(at, at, n_send.at[2, k], n_recv.at[2, k], z_nbr)
-        at = hot_at(hot_of(k), y, 1 - z, k % 3)
-        return remote(at, at, n_send.at[2, k], n_recv.at[2, k], y_nbr)
-
-    def across(k):
-        at = hot_at(hot_of(k), 1 - y, 1 - z, k % 3)
-        return remote(at, at, f_send.at[k], n_recv.at[2, k], x_nbr)
-
-    def onward_do(k, what):
-        if k < 4:
-            pl.when(c == x)(lambda: what(onward(k)))
-        else:
-            what(onward(k))
-
-    def from_diag(k):
-        at = hot_at(hot_of(k), 1 - y, 1 - z, k % 3)
-        return at, remote(at, at, q_send.at[3, k], q_recv.at[3, k], partner)
-
-    def landed(at, sem):
-        pltpu.make_async_copy(at, at, sem).wait()
-
     for load, _ in tails:
         load.start()
     for load, store in tails:
         load.wait()
         store.start()
-    for k in CH:
-        xs[k].wait_recv()
-        owner = owner_ref[2 * c + k // 3]
-        choose(owner // 2 == x, vmem(own13, own2, k), vmem(far13, far2, k), vmem(par13, par2, k))
-        if k > 0:
-            for copy in fan(k - 1):
-                copy.start()
-        spread(6 + k, 7 + k)
-    for copy in fan(5):
-        copy.start()
-    spread(12, len(homes))
-    for k in CH:
-        at, pass_on = from_y(k)
-        landed(at, n_recv.at[0, k])
-        if k % 2 == 0:
-            onward_do(k, lambda copy: copy.start())
-        pass_on.start()
-        at, pass_on = from_z(k)
-        landed(at, n_recv.at[1, k])
-        if k % 2 == 1:
-            onward_do(k, lambda copy: copy.start())
-        pass_on.start()
-    for k in CH:
-        at, pass_on = from_diag(k)
-        landed(at, n_recv.at[2, k])
-        if k < 4:
-            pl.when(c == x)(lambda: across(k).start())
-        pass_on.start()
-
     for _, store in tails:
         store.wait()
-    for k in CH:
-        dd[k].wait_send()
-        to_y, to_z, to_p, to_self = fan(k)
-        to_y.wait_send()
-        to_z.wait_send()
-        to_p.wait_send()
-        to_self.wait()
-        xs[k].wait_send()
-        onward_do(k, lambda copy: copy.wait_send())
-        if k < 4:
-            pl.when(c == x)(lambda: across(k).wait_send())
-        from_y(k)[1].wait_send()
-        from_z(k)[1].wait_send()
-        from_diag(k)[1].wait_send()
-    for k in CH:
-        h, w = 2 * (1 - c) + k // 3, k % 3
-        landed(hot_at(h, y, z, w), q_recv.at[0, k])
-        landed(hot_at(h, 1 - y, z, w), q_recv.at[1, k])
-        landed(hot_at(h, y, 1 - z, w), q_recv.at[2, k])
-        landed(hot_at(h, 1 - y, 1 - z, w), q_recv.at[3, k])
     for b in homes:
         home_sent(*b)
     for w in range(3):
@@ -294,6 +141,133 @@
                     else:
                         at = o13.at[lay, b0, :, pl.ds(half * f_loc + w * f_all, f_loc)]
                     landed(at, rg_recv.at[w, b0, lay * 2 + half])
+
+
+def hot_kernel(
+    owner_ref, pg, pu, pd, h13, h2,
+    own13, own2, par13, par2, far13, far2,
+    loc_sem, dd_send, dd_recv, x_send, x_recv, n_send, n_recv, q_send, q_recv, w_sem,
+):
+    x, y, z, c = place_of_device()
+    f_loc = pg.shape[2]
+    f_all = f_loc * 2
+    partner = (z, y, x * 2 + 1 - c)
+    x_nbr = (z, y, (1 - x) * 2 + c)
+    y_nbr = (z, 1 - y, x * 2 + c)
+    z_nbr = (1 - z, y, x * 2 + c)
+
+    def vmem(b13, b2, k):
+        return b2.at[k // 3] if k % 3 == 2 else b13.at[(k // 3) * 2 + k % 3]
+
+    def picked(h, w):
+        return (pg, pu, pd)[w].at[h]
+
+    def hot_at(h, lay, half, w):
+        if w == 2:
+            return h2.at[lay, h, pl.ds(pl.multiple_of(half * f_loc, 128), f_loc)]
+        return h13.at[lay, h, :, pl.ds(pl.multiple_of(half * f_loc + w * f_all, 128), f_loc)]
+
+    CH = range(6)
+    dd = [remote(picked(2 * (1 - c) + k // 3, k % 3), vmem(par13, par2, k), dd_send.at[k], dd_recv.at[k], partner) for k in CH]
+    own = [pltpu.make_async_copy(picked(2 * c + k // 3, k % 3), vmem(own13, own2, k), loc_sem.at[k]) for k in CH]
+    xs = [remote(vmem(own13, own2, k), vmem(far13, far2, k), x_send.at[k], x_recv.at[k], x_nbr) for k in CH]
+
+    def choose(take_a, a, b, out):
+        rows = a.shape[0] // 8
+
+        def body(i, carry):
+            at = pl.ds(pl.multiple_of(i * rows, 16), rows)
+            out[at, :] = jnp.where(take_a, a[at, :], b[at, :])
+            return carry
+
+        lax.fori_loop(0, 8, body, 0)
+
+    def hot_of(k):
+        return 2 * c + k // 3
+
+    def fan(k):
+        src, w = vmem(par13, par2, k), k % 3
+        dst = hot_at(hot_of(k), y, z, w)
+        return (
+            remote(src, dst, n_send.at[0, k], n_recv.at[0, k], y_nbr),
+            remote(src, dst, n_send.at[1, k], n_recv.at[1, k], z_nbr),
+            remote(src, dst, q_send.at[0, k], q_recv.at[0, k], partner),
+            pltpu.make_async_copy(src, dst, w_sem.at[k]),
+        )
+
+    def from_y(k):
+        at = hot_at(hot_of(k), 1 - y, z, k % 3)
+        return at, remote(at, at, q_send.at[1, k], q_recv.at[1, k], partner)
+
+    def from_z(k):
+        at = hot_at(hot_of(k), y, 1 - z, k % 3)
+        return at, remote(at, at, q_send.at[2, k], q_recv.at[2, k], partner)
+
+    def onward(k):
+        if k % 2 == 0:
+            at = hot_at(hot_of(k), 1 - y, z, k % 3)
+            return remote(at, at, n_send.at[2, k], n_recv.at[2, k], z_nbr)
+        at = hot_at(hot_of(k), y, 1 - z, k % 3)
+        return remote(at, at, n_send.at[2, k], n_recv.at[2, k], y_nbr)
+
+    def from_diag(k):
+        at = hot_at(hot_of(k), 1 - y, 1 - z, k % 3)
+        return at, remote(at, at, q_send.at[3, k], q_recv.at[3, k], partner)
+
+    for k in CH:
+        own[k].start()
+        dd[k].start()
+    for s in range(11):
+        if s < 6:
+            own[s].wait()
+            dd[s].wait_recv()
+            owner = owner_ref[2 * c + s // 3]
+            choose(owner % 2 == c, vmem(own13, own2, s), vmem(par13, par2, s), vmem(own13, own2, s))
+        if 1 <= s <= 6:
+            xs[s - 1].start()
+        k = s - 3
+        if 0 <= k < 6:
+            xs[k].wait_recv()
+            owner = owner_ref[2 * c + k // 3]
+            choose(owner // 2 == x, vmem(own13, own2, k), vmem(far13, far2, k), vmem(par13, par2, k))
+        k = s - 4
+        if 0 <= k < 6:
+            for copy in fan(k):
+                copy.start()
+    for k in CH:
+        at, pass_on = from_y(k)
+        landed(at, n_recv.at[0, k])
+        if k % 2 == 0:
+            onward(k).start()
+        pass_on.start()
+        at, pass_on = from_z(k)
+        landed(at, n_recv.at[1, k])
+        if k % 2 == 1:
+            onward(k).start()
+        pass_on.start()
+    for k in CH:
+        at, pass_on = from_diag(k)
+        landed(at, n_recv.at[2, k])
+        pass_on.start()
+
+    for k in CH:
+        dd[k].wait_send()
+        xs[k].wait_send()
+        to_y, to_z, to_p, to_self = fan(k)
+        to_y.wait_send()
+        to_z.wait_send()
+        to_p.wait_send()
+        to_self.wait()
+        onward(k).wait_send()
+        from_y(k)[1].wait_send()
+        from_z(k)[1].wait_send()
+        from_diag(k)[1].wait_send()
+    for k in CH:
+        h, w = 2 * (1 - c) + k // 3, k % 3
+        landed(hot_at(h, y, z, w), q_recv.at[0, k])
+        landed(hot_at(h, 1 - y, z, w), q_recv.at[1, k])
+        landed(hot_at(h, y, 1 - z, w), q_recv.at[2, k])
+        landed(hot_at(h, 1 - y, 1 - z, w), q_recv.at[3, k])
 
 
 def settle_kernel(o13, o2, o2b, h13, h2, q13, q2, g13, g2, buf13, buf2, sems):
@@ -414,24 +388,33 @@
         shape = lambda *dims: jax.ShapeDtypeStruct(dims, dtype)
         tail_rows = f_loc * 2 // 3
         held = pltpu.VMEM((4, tail_rows, d_model), dtype)
-        o13, o2, o2b, h13, h2, *tail = pl.pallas_call(
-            move_kernel,
+        h13, h2 = pl.pallas_call(
+            hot_kernel,
+            out_shape=[
+                shape(layers, hot, d_model, 2 * f_all),
+                shape(layers, hot, f_all, d_model),
+            ],
+            in_specs=[pl.BlockSpec(memory_space=pltpu.SMEM)] + [ANY] * 3,
+            out_specs=[ANY] * 2,
+            scratch_shapes=[
+                buf13, buf2, buf13, buf2, buf13, buf2,
+                dma((6,)), dma((6,)), dma((6,)), dma((6,)), dma((6,)),
+                dma((3, 6)), dma((3, 6)), dma((4, 6)), dma((4, 6)), dma((6,)),
+            ],
+            compiler_params=pltpu.CompilerParams(has_side_effects=True, vmem_limit_bytes=48 * 1024 * 1024),
+        )(owner, *picked)
+        o13, o2, o2b, *tail = pl.pallas_call(
+            home_kernel,
             out_shape=[
                 shape(layers, home, d_model, 2 * f_all),
                 shape(layers, f_all, d_model),
                 shape(layers, f_all - fs_size * tail_rows, d_model),
-                shape(layers, hot, d_model, 2 * f_all),
-                shape(layers, hot, f_all, d_model),
             ] + [shape(tail_rows, d_model)] * 4,
-            in_specs=[pl.BlockSpec(memory_space=pltpu.SMEM)] + [ANY] * 6,
-            out_specs=[ANY] * 9,
-            scratch_shapes=[
-                buf13, buf2, buf13, buf2, buf13, buf2, held, dma((2, 4)),
-                dma((3, 8)), dma((3, 2, 4)), dma((6,)), dma((6,)), dma((6,)), dma((6,)), dma((6,)),
-                dma((3, 6)), dma((3, 6)), dma((4,)), dma((4, 6)), dma((4, 6)), dma((6,)),
-            ],
+            in_specs=[ANY] * 3,
+            out_specs=[ANY] * 7,
+            scratch_shapes=[held, dma((2, 4)), dma((3, 8)), dma((3, 2, 4))],
             compiler_params=pltpu.CompilerParams(has_side_effects=True, vmem_limit_bytes=48 * 1024 * 1024),
-        )(owner, w_gate, w_up, w_down, *picked)
+        )(w_gate, w_up, w_down)
         moved = [lax.ppermute(t, ("fs", "pp", "ep"), tail_pairs(n)) for n, t in enumerate(tail)]
         copied = 4 * (o13.size + o2.size + h13.size + h2.size)
         q13, q2, g13, g2 = pl.pallas_call(

time: 850 us -> 1030 us (1.21)
  Pallas kernels: 827 us -> 1010 us
    pallas_call x1 -> x2, Pallas kernels: 741 us -> 923 us  [the longest x1 518 us: device_body(): pl.pallas_call(home_kernel, out_shape=[shape(layers, home, d_model, 2 * f...]
  transfers between devices with their start and end apart: 4 -> 4, of which waited for: 0 -> 0; matrix products, arithmetic and copies ran while one was open for 0% -> 0% of each run, Pallas kernels for 8% -> 48%
where the time goes in v5:
time: 1030 us; the launch traced here: 1020 us
  Pallas kernels  1010 us (98%)
    pallas_call x1, Pallas kernels, device_body(): pl.pallas_call(home_kernel, out_shape=[shape(layers, home, d_model, 2 * f...  518 us
    pallas_call x1, Pallas kernels, device_body(): pl.pallas_call(hot_kernel, out_shape=[shape(layers, hot, d_model, 2 * f_a...  405 us
    pallas_call x1, Pallas kernels, device_body(): pl.pallas_call(settle_kernel, out_shape=[shape(*o13.shape), shape(layers,...  69.6 us
  transfers between devices with their start and end apart: 4, of which 0 were waited for; matrix products, arithmetic and copies ran while one was open for 0% of the time, Pallas kernels for 48%

profile of v5, /device:TPU:2, one launch (start us, length us, event | category | flops | bytes accessed | tf_op | source)
XLA Modules:
  0.0 1020.3 jit_solution(7985358787839644032)
XLA Ops:
  0.6 0.0 copy-start.3
  0.6 518.1 %shard_map.75 = (bf16[2,2,2048,1536]{3,2,1,0:T(8,128)(2,1)}, bf16[2,768,2048]{2,1,0:T(8,128)(2,1)}, bf16[2,256,2048]{2,1,0:T(8,128)(2,1)}, bf16[256,2048]{1,0:T(...) custom-call(bf16[1,8,2048,384]{3,2,1,0:T(8,128)(2,1)} %g_ref.1, ...), custom_call_target="tpu_custom_call" | custom-call | tf_op jit(solution)/shard_map/pallas_call | solution.py:406
  518.8 0.0 copy-start.1
  518.8 0.0 copy-start.2
  518.8 1.9 collective-permute-start
  520.7 4.5 collective-permute-start.1
  525.3 0.1 collective-permute-start.2
  525.3 3.5 collective-permute-start.3
  528.8 0.0 copy-done.3
  528.9 0.5 subtract_clamp_fusion
  529.4 13.1 %shard_map.76 = (bf16[4,2048,384]{2,1,0:T(8,128)(2,1)}, bf16[4,2048,384]{2,1,0:T(8,128)(2,1)}, bf16[4,384,2048]{2,1,0:T(8,128)(2,1)}) custom-call(s32[4]{0:T(128)} %get-tuple-element.36.off_ref, bf16[1,8,2048,384]{3,2,1,0:T(8,128)(2,1)} %g_ref.1, bf16[1,8,2048,384]{3,2,1,0:T(8,128)(2,1)} %u_ref.1, bf16[1,8,384,2048]{3,2,1,0:T(8,128)(2,1)} %d_ref.1), custom_call_target="tpu_custom_call" | custom-call | tf_op jit(solution)/shard_map/pallas_call | solution.py:27
  542.4 0.0 copy-done.1
  542.4 0.0 copy-done.2
  542.5 0.0 copy-start
  542.5 404.8 %shard_map.77 = (bf16[2,4,2048,1536]{3,2,1,0:T(8,128)(2,1)}, bf16[2,4,768,2048]{3,2,1,0:T(8,128)(2,1)}) custom-call(s32[4]{0:T(128)S(1)} %get-tuple-element.37.owner_ref, bf16[4,2048,384]{2,1,0:T(8,128)(2,1)} %get-tuple-element.23.pg, bf16[4,2048,384]{2,1,0:T(8,128)(2,1)} %get-tuple-element.24.pu, bf16[4,384,2048]{2,1,0:T(8,128)(2,1)} %get-tuple-element.25.pd), custom_call_target="tpu_custom_call" | custom-call | tf_op jit(solution)/shard_map/pallas_call | solution.py:391
  947.3 0.0 copy-done
  947.3 69.6 %shard_map.78 = (bf16[2,2,2048,1536]{3,2,1,0:T(8,128)(2,1)}, bf16[2,2,768,2048]{3,2,1,0:T(8,128)(2,1)}, bf16[2,4,2048,1536]{3,2,1,0:T(8,128)(2,1)}, bf16[2,4,768,2048]{3,2,1,0:T(8,128)(2,1)}) custom-call(bf16[2,2,2048,1536]{3,2,1,0:T(8,128)(2,1)} %get-tuple-element.20.o13, bf16[2,768,2048]{2,1,0:T(8,128)(2,1)} %get-tuple-element.21.o2, ...), custom_call_target="tpu_custom_call" | custom-call | flops 1000000000 | bytes 213909504 | tf_op jit(solution)/shard_map/pallas_call | solution.py:420
  1016.9 0.0 collective-permute-done.r0
  1016.9 0.0 collective-permute-done.1.r1
  1017.0 0.0 collective-permute-done.2.r2
  1017.0 0.0 collective-permute-done.3.r3
  1017.0 3.3 shard_map.79
Async XLA Ops:
  0.6 528.2 %copy-start.3 = (s32[4]{0:T(128)S(1)}, s32[4]{0:T(128)}, u32[]{:S(2)}) copy-start(s32[4]{0:T(128)} %param.7) | copy-start | bytes 52
  518.8 23.7 %copy-start.1 = (bf16[256,2048]{1,0:T(8,128)(2,1)}, bf16[256,2048]{1,0:T(8,128)(2,1)S(1)}, u32[]{:S(2)}) copy-start(bf16[256,2048]{1,0:T(8,128)(2,1)S(1)} %get-tuple-element.29.t0) | copy-start | bytes 3145732
  518.8 23.7 %copy-start.2 = (bf16[256,2048]{1,0:T(8,128)(2,1)}, bf16[256,2048]{1,0:T(8,128)(2,1)S(1)}, u32[]{:S(2)}) copy-start(bf16[256,2048]{1,0:T(8,128)(2,1)S(1)} %get-tuple-element.30.t1) | copy-start | bytes 3145732
  518.8 498.2 %collective-permute-start = (bf16[256,2048]{1,0:T(8,128)(2,1)S(1)}, bf16[256,2048]{1,0:T(8,128)(2,1)}, u32[]{:S(2)}, u32[]{:S(2)}) collective-permute-start(bf16[256,2048]{1,0:T(8,128)(2,1)S(1)} %get-tuple-element.29.t0), channel_id=1, source_target_pairs={{1,3},{2,4},{3,7},{4,1},{5,2},{6,5},{7,6},{9,11},{10,12},{11,15},{... | collective-permute-start | bytes 3145736 | tf_op jit(solution)/shard_map/ppermute | solution.py:418
  520.7 496.2 %collective-permute-start.1 = (bf16[256,2048]{1,0:T(8,128)(2,1)S(1)}, bf16[256,2048]{1,0:T(8,128)(2,1)}, u32[]{:S(2)}, u32[]{:S(2)}) collective-permute-start(bf16[256,2048]{1,0:T(8,128)(2,1)S(1)} %get-tuple-element.30.t1), channel_id=1, source_target_pairs={{0,1},{1,2},{2,5},{3,6},{4,0},{5,3},{6,4},{8,9},{9,10},{10,13},{11... | collective-permute-start | bytes 3145736 | tf_op jit(solution)/shard_map/ppermute | solution.py:418
  525.3 491.7 %collective-permute-start.2 = (bf16[256,2048]{1,0:T(8,128)(2,1)}, bf16[256,2048]{1,0:T(8,128)(2,1)}, u32[]{:S(2)}, u32[]{:S(2)}) collective-permute-start(bf16[256,2048]{1,0:T(8,128)(2,1)} %get-tuple-element.31), channel_id=1, source_target_pairs={{0,8},{1,11},{2,12},{3,15},{4,9},{5,10},{6,13},{7,14},{8,0},{9,3},... | collective-permute-start | bytes 3145736 | tf_op jit(solution)/shard_map/ppermute | solution.py:418
  525.3 491.7 %collective-permute-start.3 = (bf16[256,2048]{1,0:T(8,128)(2,1)S(1)}, bf16[256,2048]{1,0:T(8,128)(2,1)}, u32[]{:S(2)}, u32[]{:S(2)}) collective-permute-start(bf16[256,2048]{1,0:T(8,128)(2,1)S(1)} %get-tuple-element.32), channel_id=1, source_target_pairs={{0,9},{1,10},{2,13},{3,14},{4,8},{5,11},{6,12},{7,15},{8,1},{9,2},... | collective-permute-start | bytes 3145736 | tf_op jit(solution)/shard_map/ppermute | solution.py:418
  542.5 404.8 %copy-start = (bf16[2,256,2048]{2,1,0:T(8,128)(2,1)S(1)}, bf16[2,256,2048]{2,1,0:T(8,128)(2,1)}, u32[]{:S(2)}) copy-start(bf16[2,256,2048]{2,1,0:T(8,128)(2,1)} %get-tuple-element.22.o2b) | copy-start | bytes 6291460

commit v6 on v4

--- a/solution.py
+++ b/solution.py
@@ -84,8 +84,8 @@
 
     stays = (x == y) & (c == x)
 
-    def home_refs(j, i, b0, w):
-        b1, b2 = (z + i) % 2, (c + j) % 2
+    def home_refs(j, n, b0, w):
+        b1, b2 = (z + n + 1 + x + y) % 2, (c + j) % 2
         src = (wg, wu, wd)[w].at[0, 4 * b2 + 2 * b1 + b0]
         if w == 2 and b0 == 1:
             src = src.at[pl.ds(tail_rows, kept)]
@@ -96,36 +96,36 @@
             dst = o13.at[y, b0, :, cols(z, w)]
         return src, dst, rg_recv.at[w, b0, y * 2 + z], (b1, x, c * 2 + b2)
 
-    def home_copy(j, i, b0, w):
-        src, dst, recv, dev = home_refs(j, i, b0, w)
-        return remote(src, dst, rg_send.at[w, 4 * j + 2 * i + b0], recv, dev)
-
-    def home_start(j, i, b0, w):
-        if (j, i) != (0, 0):
-            home_copy(j, i, b0, w).start()
+    def home_copy(j, n, b0, w):
+        src, dst, recv, dev = home_refs(j, n, b0, w)
+        return remote(src, dst, rg_send.at[w, 4 * j + 2 * n + b0], recv, dev)
+
+    def home_start(j, n, b0, w):
+        if (j, n) != (0, 1):
+            home_copy(j, n, b0, w).start()
             return
 
         @pl.when(stays)
         def _():
-            src, dst, recv, _ = home_refs(j, i, b0, w)
+            src, dst, recv, _ = home_refs(j, n, b0, w)
             pltpu.make_async_copy(src, dst, recv).start()
 
         @pl.when(jnp.logical_not(stays))
         def _():
-            home_copy(j, i, b0, w).start()
-
-    def home_sent(j, i, b0, w):
-        if (j, i) != (0, 0):
-            home_copy(j, i, b0, w).wait_send()
+            home_copy(j, n, b0, w).start()
+
+    def home_sent(j, n, b0, w):
+        if (j, n) != (0, 1):
+            home_copy(j, n, b0, w).wait_send()
             return
 
         @pl.when(jnp.logical_not(stays))
         def _():
-            home_copy(j, i, b0, w).wait_send()
+            home_copy(j, n, b0, w).wait_send()
 
     homes = [
-        (j, i, b0, w)
-        for b0 in range(2) for w in range(3) for j in range(2) for i in range(2)
+        (j, n, b0, w)
+        for n in range(2) for b0 in range(2) for w in range(3) for j in range(2)
     ]
 
     tails = []
@@ -154,7 +154,7 @@
     for k in CH:
         own[k].start()
         dd[k].start()
-    for b in homes[:2]:
+    for b in homes[:4]:
         home_start(*b)
     for k in CH:
         own[k].wait()
@@ -163,8 +163,8 @@
         choose(owner % 2 == c, vmem(own13, own2, k), vmem(par13, par2, k), vmem(own13, own2, k))
         if k > 0:
             xs[k - 1].start()
-    for b in homes[2:4]:
-        home_start(*b)
+    for load, _ in tails:
+        load.start()
     xs[5].start()
 
     @pl.when(c != x)
@@ -213,7 +213,7 @@
         return remote(at, at, f_send.at[k], n_recv.at[2, k], x_nbr)
 
     def onward_do(k, what):
-        if k < 4:
+        if k < 2:
             pl.when(c == x)(lambda: what(onward(k)))
         else:
             what(onward(k))
@@ -225,8 +225,6 @@
     def landed(at, sem):
         pltpu.make_async_copy(at, at, sem).wait()
 
-    for load, _ in tails:
-        load.start()
     for load, store in tails:
         load.wait()
         store.start()
@@ -237,10 +235,9 @@
         if k > 0:
             for copy in fan(k - 1):
                 copy.start()
-        spread(6 + k, 7 + k)
     for copy in fan(5):
         copy.start()
-    spread(12, len(homes))
+    spread(6, 8)
     for k in CH:
         at, pass_on = from_y(k)
         landed(at, n_recv.at[0, k])
@@ -252,10 +249,12 @@
         if k % 2 == 1:
             onward_do(k, lambda copy: copy.start())
         pass_on.start()
+        spread(8 + k, 9 + k)
+    spread(14, len(homes))
     for k in CH:
         at, pass_on = from_diag(k)
         landed(at, n_recv.at[2, k])
-        if k < 4:
+        if k < 2:
             pl.when(c == x)(lambda: across(k).start())
         pass_on.start()
 
@@ -270,7 +269,7 @@
         to_self.wait()
         xs[k].wait_send()
         onward_do(k, lambda copy: copy.wait_send())
-        if k < 4:
+        if k < 2:
             pl.when(c == x)(lambda: across(k).wait_send())
         from_y(k)[1].wait_send()
         from_z(k)[1].wait_send()

time: 850 us -> 953 us (1.12)
  starting transfers between devices: 15.5 us -> 137 us
  Pallas kernels: 827 us -> 809 us
    ppermute x4, starting transfers between devices: 15.5 us -> 137 us  [device_body(): lax.ppermute(t, ('fs', 'pp', 'ep'), tail_pairs(n))]
    pallas_call x1, Pallas kernels: 741 us -> 723 us  [device_body(): pl.pallas_call(move_kernel, out_shape=[shape(layers, home, d_model, 2 * f...]
  transfers between devices with their start and end apart: 4 -> 4, of which waited for: 0 -> 0; matrix products, arithmetic and copies ran while one was open for 0% -> 0% of each run, Pallas kernels for 8% -> 7%
where the time goes in v6:
time: 953 us; the launch traced here: 951 us
  Pallas kernels  809 us (85%)
  starting transfers between devices  137 us (14%)
    pallas_call x1, Pallas kernels, device_body(): pl.pallas_call(move_kernel, out_shape=[shape(layers, home, d_model, 2 * f...  723 us
    ppermute x4, starting transfers between devices, device_body(): lax.ppermute(t, ('fs', 'pp', 'ep'), tail_pairs(n))  137 us
    pallas_call x1, Pallas kernels, device_body(): pl.pallas_call(settle_kernel, out_shape=[shape(*o13.shape), shape(layers,...  69.6 us
  transfers between devices with their start and end apart: 4, of which 0 were waited for; matrix products, arithmetic and copies ran while one was open for 0% of the time, Pallas kernels for 7%

profile of v6, /device:TPU:2, one launch (start us, length us, event | category | flops | bytes accessed | tf_op | source)
XLA Modules:
  0.0 951.3 jit_solution(10384523436663652699)
XLA Ops:
  0.6 1.2 subtract_clamp_fusion
  1.8 13.0 %shard_map.75 = (bf16[4,2048,384]{2,1,0:T(8,128)(2,1)}, bf16[4,2048,384]{2,1,0:T(8,128)(2,1)}, bf16[4,384,2048]{2,1,0:T(8,128)(2,1)}) custom-call(s32[4]{0:T(128)} %get-tuple-element.36.off_ref, bf16[1,8,2048,384]{3,2,1,0:T(8,128)(2,1)} %wg.1, bf16[1,8,2048,384]{3,2,1,0:T(8,128)(2,1)} %wu.1, bf16[1,8,384,2048]{3,2,1,0:T(8,128)(2,1)} %wd.1), custom_call_target="tpu_custom_call" | custom-call | tf_op jit(solution)/shard_map/pallas_call | solution.py:27
  14.8 722.8 %shard_map.76 = (bf16[2,2,2048,1536]{3,2,1,0:T(8,128)(2,1)}, bf16[2,768,2048]{2,1,0:T(8,128)(2,1)}, bf16[2,256,2048]{2,1,0:T(8,128)(2,1)}, bf16[2,4,2048,1536]{3...) custom-call(s32[4]{0:T(128)S(1)} %get-tuple-element.37.owner_ref, ...), custom_call_target="tpu_custom_call" | custom-call | tf_op jit(solution)/shard_map/pallas_call | solution.py:416
  737.6 0.0 copy-start.1
  737.6 0.0 copy-start.2
  737.7 131.6 %collective-permute-start = (bf16[256,2048]{1,0:T(8,128)(2,1)S(1)}, bf16[256,2048]{1,0:T(8,128)(2,1)S(1)}, u32[]{:S(2)}, u32[]{:S(2)}) collective-permute-start(bf16[256,2048]{1,0:T(8,128)(2,1)S(1)} %get-tuple-element.29.t0), channel_id=1, source_target_pairs={{1,3},{2,4},{3,7},{4,1},{5,2},{6,5},{7,6},{9,11},{10,12},{11,15},{... | collective-permute-start | bytes 3145736 | tf_op jit(solution)/shard_map/ppermute | solution.py:434
  869.3 1.9 collective-permute-start.1
  871.2 2.8 collective-permute-start.2
  874.0 0.8 collective-permute-start.3
  874.8 0.0 copy-start
  874.8 1.6 copy-done
  876.4 69.6 %shard_map.77 = (bf16[2,2,2048,1536]{3,2,1,0:T(8,128)(2,1)}, bf16[2,2,768,2048]{3,2,1,0:T(8,128)(2,1)}, bf16[2,4,2048,1536]{3,2,1,0:T(8,128)(2,1)}, bf16[2,4,768,2048]{3,2,1,0:T(8,128)(2,1)}) custom-call(bf16[2,2,2048,1536]{3,2,1,0:T(8,128)(2,1)} %get-tuple-element.23.o13, bf16[2,768,2048]{2,1,0:T(8,128)(2,1)} %get-tuple-element.24.o2, ...), custom_call_target="tpu_custom_call" | custom-call | flops 1000000000 | bytes 213909504 | tf_op jit(solution)/shard_map/pallas_call | solution.py:436
  946.0 0.0 copy-done.1
  946.0 0.0 copy-done.2
  946.0 0.0 collective-permute-done.r0
  946.0 0.0 copy-start.3
  946.0 0.0 collective-permute-done.1.r1
  946.1 0.0 copy-start.4
  946.1 0.0 collective-permute-done.2.r2
  946.1 0.0 copy-start.5
  946.1 0.0 collective-permute-done.3.r3
  946.1 0.0 copy-start.6
  946.1 1.0 copy-done.6
  947.1 0.2 copy-done.3
  947.4 0.4 copy-done.4
  947.7 0.3 copy-done.5
  948.0 3.3 shard_map.78
Async XLA Ops:
  737.6 208.4 %copy-start.1 = (bf16[256,2048]{1,0:T(8,128)(2,1)}, bf16[256,2048]{1,0:T(8,128)(2,1)S(1)}, u32[]{:S(2)}) copy-start(bf16[256,2048]{1,0:T(8,128)(2,1)S(1)} %get-tuple-element.29.t0) | copy-start | bytes 3145732
  737.6 208.4 %copy-start.2 = (bf16[256,2048]{1,0:T(8,128)(2,1)}, bf16[256,2048]{1,0:T(8,128)(2,1)S(1)}, u32[]{:S(2)}) copy-start(bf16[256,2048]{1,0:T(8,128)(2,1)S(1)} %get-tuple-element.30.t1) | copy-start | bytes 3145732
  737.7 208.4 %collective-permute-start = (bf16[256,2048]{1,0:T(8,128)(2,1)S(1)}, bf16[256,2048]{1,0:T(8,128)(2,1)S(1)}, u32[]{:S(2)}, u32[]{:S(2)}) collective-permute-start(bf16[256,2048]{1,0:T(8,128)(2,1)S(1)} %get-tuple-element.29.t0), channel_id=1, source_target_pairs={{1,3},{2,4},{3,7},{4,1},{5,2},{6,5},{7,6},{9,11},{10,12},{11,15},{... | collective-permute-start | bytes 3145736 | tf_op jit(solution)/shard_map/ppermute | solution.py:434
  869.3 76.8 %collective-permute-start.1 = (bf16[256,2048]{1,0:T(8,128)(2,1)S(1)}, bf16[256,2048]{1,0:T(8,128)(2,1)S(1)}, u32[]{:S(2)}, u32[]{:S(2)}) collective-permute-start(bf16[256,2048]{1,0:T(8,128)(2,1)S(1)} %get-tuple-element.30.t1), channel_id=1, source_target_pairs={{0,1},{1,2},{2,5},{3,6},{4,0},{5,3},{6,4},{8,9},{9,10},{10,13},{11... | collective-permute-start | bytes 3145736 | tf_op jit(solution)/shard_map/ppermute | solution.py:434
  871.2 74.9 %collective-permute-start.2 = (bf16[256,2048]{1,0:T(8,128)(2,1)S(1)}, bf16[256,2048]{1,0:T(8,128)(2,1)S(1)}, u32[]{:S(2)}, u32[]{:S(2)}) collective-permute-start(bf16[256,2048]{1,0:T(8,128)(2,1)S(1)} %get-tuple-element.31), channel_id=1, source_target_pairs={{0,8},{1,11},{2,12},{3,15},{4,9},{5,10},{6,13},{7,14},{8,0},{9,3},... | collective-permute-start | bytes 3145736 | tf_op jit(solution)/shard_map/ppermute | solution.py:434
  874.0 72.1 %collective-permute-start.3 = (bf16[256,2048]{1,0:T(8,128)(2,1)S(1)}, bf16[256,2048]{1,0:T(8,128)(2,1)S(1)}, u32[]{:S(2)}, u32[]{:S(2)}) collective-permute-start(bf16[256,2048]{1,0:T(8,128)(2,1)S(1)} %get-tuple-element.32), channel_id=1, source_target_pairs={{0,9},{1,10},{2,13},{3,14},{4,8},{5,11},{6,12},{7,15},{8,1},{9,2},... | collective-permute-start | bytes 3145736 | tf_op jit(solution)/shard_map/ppermute | solution.py:434
  874.8 1.6 copy-start
  946.0 1.3 copy-start.3
  946.1 1.7 copy-start.4
  946.1 1.9 copy-start.5
  946.1 1.0 copy-start.6

commit v7 on v4

--- a/solution.py
+++ b/solution.py
@@ -11,44 +11,11 @@
 ANY = pl.BlockSpec(memory_space=pl.ANY)
 
 
-def pick_kernel(off_ref, g_ref, u_ref, d_ref, pg_ref, pu_ref, pd_ref):
-    pg_ref[...] = g_ref[0]
-    pu_ref[...] = u_ref[0]
-    pd_ref[...] = d_ref[0]
-
-
-def pick_hot(w_gate, w_up, w_down, offset):
-    hot = offset.shape[0]
-    _, _, d_model, f_loc = w_gate.shape
-    take_in = lambda h, off: (0, off[h], 0, 0)
-    put = lambda h, off: (h, 0, 0)
-    shape_in = jax.ShapeDtypeStruct((hot, d_model, f_loc), w_gate.dtype)
-    shape_down = jax.ShapeDtypeStruct((hot, f_loc, d_model), w_gate.dtype)
-    return pl.pallas_call(
-        pick_kernel,
-        grid_spec=pltpu.PrefetchScalarGridSpec(
-            num_scalar_prefetch=1,
-            grid=(hot,),
-            in_specs=[
-                pl.BlockSpec((1, 1, d_model, f_loc), take_in),
-                pl.BlockSpec((1, 1, d_model, f_loc), take_in),
-                pl.BlockSpec((1, 1, f_loc, d_model), take_in),
-            ],
-            out_specs=[
-                pl.BlockSpec((1, d_model, f_loc), put),
-                pl.BlockSpec((1, d_model, f_loc), put),
-                pl.BlockSpec((1, f_loc, d_model), put),
-            ],
-        ),
-        out_shape=[shape_in, shape_in, shape_down],
-    )(offset, w_gate, w_up, w_down)
-
-
 def move_kernel(
-    owner_ref, wg, wu, wd, pg, pu, pd, o13, o2, o2b, h13, h2, t0, t1, t2, t3,
-    own13, own2, par13, par2, far13, far2, held, t_sem,
+    owner_ref, off_ref, wg, wu, wd, o13, o2, o2b, h13, h2, t0, t1, t2, t3,
+    all13, all2, give13, give2, own13, own2, par13, par2, far13, far2, t_sem,
     rg_send, rg_recv, loc_sem, dd_send, dd_recv, x_send, x_recv,
-    n_send, n_recv, f_send, q_send, q_recv, w_sem,
+    n_send, n_recv, q_send, q_recv, w_sem,
 ):
     z = lax.axis_index("fs")
     y = lax.axis_index("pp")
@@ -74,9 +41,6 @@
     def vmem(b13, b2, k):
         return b2.at[k // 3] if k % 3 == 2 else b13.at[(k // 3) * 2 + k % 3]
 
-    def picked(h, w):
-        return (pg, pu, pd)[w].at[h]
-
     def hot_at(h, lay, half, w):
         if w == 2:
             return h2.at[lay, h, pl.ds(pl.multiple_of(half * f_loc, 128), f_loc)]
@@ -131,14 +95,11 @@
     tails = []
     for n in range(4):
         e = 4 * ((c + y + n % 2) % 2) + 2 * ((z + n // 2) % 2) + 1
-        tails.append((
-            pltpu.make_async_copy(wd.at[0, e, pl.ds(0, tail_rows)], held.at[n], t_sem.at[0, n]),
-            pltpu.make_async_copy(held.at[n], (t0, t1, t2, t3)[n], t_sem.at[1, n]),
-        ))
+        tails.append(pltpu.make_async_copy(wd.at[0, e, pl.ds(0, tail_rows)], (t0, t1, t2, t3)[n], t_sem.at[n]))
 
     CH = range(6)
-    dd = [remote(picked(2 * (1 - c) + k // 3, k % 3), vmem(par13, par2, k), dd_send.at[k], dd_recv.at[k], partner) for k in CH]
-    own = [pltpu.make_async_copy(picked(2 * c + k // 3, k % 3), vmem(own13, own2, k), loc_sem.at[k]) for k in CH]
+    ORDER = (0, 3, 2, 5, 1, 4)
+    dd = [remote(vmem(give13, give2, k), vmem(par13, par2, k), dd_send.at[k], dd_recv.at[k], partner) for k in CH]
     xs = [remote(vmem(own13, own2, k), vmem(far13, far2, k), x_send.at[k], x_recv.at[k], x_nbr) for k in CH]
 
     def choose(take_a, a, b, out):
@@ -151,34 +112,57 @@
 
         lax.fori_loop(0, 8, body, 0)
 
-    for k in CH:
-        own[k].start()
-        dd[k].start()
+    def take(held, h, out):
+        rows = out.shape[0] // 8
+
+        def body(i, carry):
+            at = pl.ds(pl.multiple_of(i * rows, 16), rows)
+            out[at, :] = held[off_ref[h], at, :]
+            return carry
+
+        lax.fori_loop(0, 8, body, 0)
+
+    def take_all(w):
+        held = all2 if w == 2 else all13
+        for k in (w, 3 + w):
+            take(held, 2 * (1 - c) + k // 3, vmem(give13, give2, k))
+            take(held, 2 * c + k // 3, vmem(own13, own2, k))
+
+    gates = pltpu.make_async_copy(wg.at[0], all13, loc_sem.at[0])
+    ups = pltpu.make_async_copy(wu.at[0], all13, loc_sem.at[1])
+    downs = pltpu.make_async_copy(wd.at[0], all2, loc_sem.at[2])
+    gates.start()
     for b in homes[:2]:
         home_start(*b)
-    for k in CH:
-        own[k].wait()
+    downs.start()
+    gates.wait()
+    take_all(0)
+    ups.start()
+    downs.wait()
+    take_all(2)
+    for k in (0, 3):
+        dd[k].start()
+    ups.wait()
+    take_all(1)
+    for k in (2, 5):
+        dd[k].start()
+    for copy in tails:
+        copy.start()
+    for k in (1, 4):
+        dd[k].start()
+
+    for n in CH:
+        k = ORDER[n]
         dd[k].wait_recv()
         owner = owner_ref[2 * c + k // 3]
         choose(owner % 2 == c, vmem(own13, own2, k), vmem(par13, par2, k), vmem(own13, own2, k))
-        if k > 0:
-            xs[k - 1].start()
+        if n > 0:
+            xs[ORDER[n - 1]].start()
     for b in homes[2:4]:
         home_start(*b)
-    xs[5].start()
-
-    @pl.when(c != x)
-    def _():
-        for b in homes[4:]:
-            home_start(*b)
-
-    def spread(first, stop):
-        @pl.when(c == x)
-        def _():
-            for b in homes[first:stop]:
-                home_start(*b)
-
-    spread(4, 6)
+    xs[ORDER[5]].start()
+    for b in homes[4:]:
+        home_start(*b)
 
     def hot_of(k):
         return 2 * c + k // 3
@@ -208,16 +192,6 @@
         at = hot_at(hot_of(k), y, 1 - z, k % 3)
         return remote(at, at, n_send.at[2, k], n_recv.at[2, k], y_nbr)
 
-    def across(k):
-        at = hot_at(hot_of(k), 1 - y, 1 - z, k % 3)
-        return remote(at, at, f_send.at[k], n_recv.at[2, k], x_nbr)
-
-    def onward_do(k, what):
-        if k < 4:
-            pl.when(c == x)(lambda: what(onward(k)))
-        else:
-            what(onward(k))
-
     def from_diag(k):
         at = hot_at(hot_of(k), 1 - y, 1 - z, k % 3)
         return at, remote(at, at, q_send.at[3, k], q_recv.at[3, k], partner)
@@ -225,42 +199,36 @@
     def landed(at, sem):
         pltpu.make_async_copy(at, at, sem).wait()
 
-    for load, _ in tails:
-        load.start()
-    for load, store in tails:
-        load.wait()
-        store.start()
-    for k in CH:
+    for n in CH:
+        k = ORDER[n]
         xs[k].wait_recv()
         owner = owner_ref[2 * c + k // 3]
         choose(owner // 2 == x, vmem(own13, own2, k), vmem(far13, far2, k), vmem(par13, par2, k))
-        if k > 0:
-            for copy in fan(k - 1):
+        if n > 0:
+            for copy in fan(ORDER[n - 1]):
                 copy.start()
-        spread(6 + k, 7 + k)
-    for copy in fan(5):
+    for k in CH:
+        xs[k].wait_send()
+    for copy in fan(ORDER[5]):
         copy.start()
-    spread(12, len(homes))
-    for k in CH:
+    for k in ORDER:
         at, pass_on = from_y(k)
         landed(at, n_recv.at[0, k])
         if k % 2 == 0:
-            onward_do(k, lambda copy: copy.start())
+            onward(k).start()
         pass_on.start()
         at, pass_on = from_z(k)
         landed(at, n_recv.at[1, k])
         if k % 2 == 1:
-            onward_do(k, lambda copy: copy.start())
+            onward(k).start()
         pass_on.start()
-    for k in CH:
+    for k in ORDER:
         at, pass_on = from_diag(k)
         landed(at, n_recv.at[2, k])
-        if k < 4:
-            pl.when(c == x)(lambda: across(k).start())
         pass_on.start()
 
-    for _, store in tails:
-        store.wait()
+    for copy in tails:
+        copy.wait()
     for k in CH:
         dd[k].wait_send()
         to_y, to_z, to_p, to_self = fan(k)
@@ -268,10 +236,7 @@
         to_z.wait_send()
         to_p.wait_send()
         to_self.wait()
-        xs[k].wait_send()
-        onward_do(k, lambda copy: copy.wait_send())
-        if k < 4:
-            pl.when(c == x)(lambda: across(k).wait_send())
+        onward(k).wait_send()
         from_y(k)[1].wait_send()
         from_z(k)[1].wait_send()
         from_diag(k)[1].wait_send()
@@ -407,7 +372,6 @@
         home = exp_local // (fs_size * pp_size)
         offset = jnp.clip(hot_ids - lax.axis_index("ep") * exp_local, 0, exp_local - 1)
         owner = hot_ids // exp_local
-        picked = pick_hot(w_gate, w_up, w_down, offset)
         dma = pltpu.SemaphoreType.DMA
         buf13 = pltpu.VMEM((4, d_model, f_loc), dtype)
         buf2 = pltpu.VMEM((2, f_loc, d_model), dtype)
@@ -423,15 +387,16 @@
                 shape(layers, hot, d_model, 2 * f_all),
                 shape(layers, hot, f_all, d_model),
             ] + [shape(tail_rows, d_model)] * 4,
-            in_specs=[pl.BlockSpec(memory_space=pltpu.SMEM)] + [ANY] * 6,
+            in_specs=[pl.BlockSpec(memory_space=pltpu.SMEM)] * 2 + [ANY] * 3,
             out_specs=[ANY] * 9,
             scratch_shapes=[
-                buf13, buf2, buf13, buf2, buf13, buf2, held, dma((2, 4)),
-                dma((3, 8)), dma((3, 2, 4)), dma((6,)), dma((6,)), dma((6,)), dma((6,)), dma((6,)),
-                dma((3, 6)), dma((3, 6)), dma((4,)), dma((4, 6)), dma((4, 6)), dma((6,)),
+                pltpu.VMEM((exp_local, d_model, f_loc), dtype), pltpu.VMEM((exp_local, f_loc, d_model), dtype),
+                buf13, buf2, buf13, buf2, buf13, buf2, buf13, buf2, dma((4,)),
+                dma((3, 8)), dma((3, 2, 4)), dma((3,)), dma((6,)), dma((6,)), dma((6,)), dma((6,)),
+                dma((3, 6)), dma((3, 6)), dma((4, 6)), dma((4, 6)), dma((6,)),
             ],
-            compiler_params=pltpu.CompilerParams(has_side_effects=True, vmem_limit_bytes=48 * 1024 * 1024),
-        )(owner, w_gate, w_up, w_down, *picked)
+            compiler_params=pltpu.CompilerParams(has_side_effects=True, vmem_limit_bytes=67043328),
+        )(owner, offset, w_gate, w_up, w_down)
         moved = [lax.ppermute(t, ("fs", "pp", "ep"), tail_pairs(n)) for n, t in enumerate(tail)]
         copied = 4 * (o13.size + o2.size + h13.size + h2.size)
         q13, q2, g13, g2 = pl.pallas_call(

time: 850 us -> 831 us (0.978)
  Pallas kernels: 827 us -> 815 us
    pallas_call x1 -> x0, Pallas kernels: 13.1 us -> none  [pick_hot(): pl.pallas_call(pick_kernel, grid_spec=pltpu.PrefetchScalarGridSpec(num_sc...]
where the time goes in v7:
time: 831 us
  Pallas kernels  815 us (98%)
  starting transfers between devices  10 us (1%)
    pallas_call x1, Pallas kernels, device_body(): pl.pallas_call(move_kernel, out_shape=[shape(layers, home, d_model, 2 * f...  742 us
    pallas_call x1, Pallas kernels, device_body(): pl.pallas_call(settle_kernel, out_shape=[shape(*o13.shape), shape(layers,...  69.6 us
  transfers between devices with their start and end apart: 4, of which 0 were waited for; matrix products, arithmetic and copies ran while one was open for 0% of the time, Pallas kernels for 8%

profile of v7, /device:TPU:2, one launch (start us, length us, event | category | flops | bytes accessed | tf_op | source)
XLA Modules:
  0.0 830.6 jit_solution(4778407734344992478)
XLA Ops:
  0.6 1.2 subtract_clamp_fusion
  1.8 742.2 %shard_map.75 = (bf16[2,2,2048,1536]{3,2,1,0:T(8,128)(2,1)}, bf16[2,768,2048]{2,1,0:T(8,128)(2,1)}, bf16[2,256,2048]{2,1,0:T(8,128)(2,1)}, bf16[2,4,2048,1536]{3...) custom-call(s32[4]{0:T(128)} %get-tuple-element.31.owner_ref, ...), custom_call_target="tpu_custom_call" | custom-call | tf_op jit(solution)/shard_map/pallas_call | solution.py:381
  744.1 2.9 collective-permute-start
  747.0 3.5 collective-permute-start.1
  750.5 0.1 collective-permute-start.2
  750.6 3.5 collective-permute-start.3
  754.1 0.0 copy-start
  754.1 1.6 copy-done
  755.7 69.6 %shard_map.76 = (bf16[2,2,2048,1536]{3,2,1,0:T(8,128)(2,1)}, bf16[2,2,768,2048]{3,2,1,0:T(8,128)(2,1)}, bf16[2,4,2048,1536]{3,2,1,0:T(8,128)(2,1)}, bf16[2,4,768,2048]{3,2,1,0:T(8,128)(2,1)}) custom-call(bf16[2,2,2048,1536]{3,2,1,0:T(8,128)(2,1)} %get-tuple-element.17.o13, bf16[2,768,2048]{2,1,0:T(8,128)(2,1)} %get-tuple-element.18.o2, ...), custom_call_target="tpu_custom_call" | custom-call | flops 1000000000 | bytes 213909504 | tf_op jit(solution)/shard_map/pallas_call | solution.py:402
  825.4 0.0 collective-permute-done.r0
  825.4 0.0 copy-start.1
  825.4 0.0 collective-permute-done.1.r1
  825.4 0.0 copy-start.2
  825.4 0.0 collective-permute-done.2.r2
  825.4 0.0 copy-start.3
  825.4 0.0 collective-permute-done.3.r3
  825.4 0.0 copy-start.4
  825.4 0.9 copy-done.1
  826.3 0.4 copy-done.2
  826.7 0.3 copy-done.3
  827.0 0.3 copy-done.4
  827.3 3.3 shard_map.77
Async XLA Ops:
  744.1 81.3 %collective-permute-start = (bf16[256,2048]{1,0:T(8,128)(2,1)}, bf16[256,2048]{1,0:T(8,128)(2,1)S(1)}, u32[]{:S(2)}, u32[]{:S(2)}) collective-permute-start(bf16[256,2048]{1,0:T(8,128)(2,1)} %get-tuple-element.23.t0), channel_id=1, source_target_pairs={{1,3},{2,4},{3,7},{4,1},{5,2},{6,5},{7,6},{9,11},{10,12},{11,15},{... | collective-permute-start | bytes 3145736 | tf_op jit(solution)/shard_map/ppermute | solution.py:400
  747.0 78.4 %collective-permute-start.1 = (bf16[256,2048]{1,0:T(8,128)(2,1)}, bf16[256,2048]{1,0:T(8,128)(2,1)S(1)}, u32[]{:S(2)}, u32[]{:S(2)}) collective-permute-start(bf16[256,2048]{1,0:T(8,128)(2,1)} %get-tuple-element.24.t1), channel_id=1, source_target_pairs={{0,1},{1,2},{2,5},{3,6},{4,0},{5,3},{6,4},{8,9},{9,10},{10,13},{11... | collective-permute-start | bytes 3145736 | tf_op jit(solution)/shard_map/ppermute | solution.py:400
  750.5 74.9 %collective-permute-start.2 = (bf16[256,2048]{1,0:T(8,128)(2,1)}, bf16[256,2048]{1,0:T(8,128)(2,1)S(1)}, u32[]{:S(2)}, u32[]{:S(2)}) collective-permute-start(bf16[256,2048]{1,0:T(8,128)(2,1)} %get-tuple-element.25), channel_id=1, source_target_pairs={{0,8},{1,11},{2,12},{3,15},{4,9},{5,10},{6,13},{7,14},{8,0},{9,3},... | collective-permute-start | bytes 3145736 | tf_op jit(solution)/shard_map/ppermute | solution.py:400
  750.6 74.8 %collective-permute-start.3 = (bf16[256,2048]{1,0:T(8,128)(2,1)}, bf16[256,2048]{1,0:T(8,128)(2,1)S(1)}, u32[]{:S(2)}, u32[]{:S(2)}) collective-permute-start(bf16[256,2048]{1,0:T(8,128)(2,1)} %get-tuple-element.26), channel_id=1, source_target_pairs={{0,9},{1,10},{2,13},{3,14},{4,8},{5,11},{6,12},{7,15},{8,1},{9,2},... | collective-permute-start | bytes 3145736 | tf_op jit(solution)/shard_map/ppermute | solution.py:400
  754.1 1.6 copy-start
  825.4 1.0 copy-start.1
  825.4 1.3 copy-start.2
  825.4 1.6 copy-start.3
  825.4 1.9 copy-start.4

commit v8 on v7

--- a/solution.py
+++ b/solution.py
@@ -15,7 +15,7 @@
     owner_ref, off_ref, wg, wu, wd, o13, o2, o2b, h13, h2, t0, t1, t2, t3,
     all13, all2, give13, give2, own13, own2, par13, par2, far13, far2, t_sem,
     rg_send, rg_recv, loc_sem, dd_send, dd_recv, x_send, x_recv,
-    n_send, n_recv, q_send, q_recv, w_sem,
+    n_send, n_recv, f_send, q_send, q_recv, w_sem,
 ):
     z = lax.axis_index("fs")
     y = lax.axis_index("pp")
@@ -192,6 +192,18 @@
         at = hot_at(hot_of(k), y, 1 - z, k % 3)
         return remote(at, at, n_send.at[2, k], n_recv.at[2, k], y_nbr)
 
+    ACROSS = (0, 3)
+
+    def across(k):
+        at = hot_at(hot_of(k), 1 - y, 1 - z, k % 3)
+        return remote(at, at, f_send.at[k], n_recv.at[2, k], x_nbr)
+
+    def onward_do(k, what):
+        if k in ACROSS:
+            pl.when(c == x)(lambda: what(onward(k)))
+        else:
+            what(onward(k))
+
     def from_diag(k):
         at = hot_at(hot_of(k), 1 - y, 1 - z, k % 3)
         return at, remote(at, at, q_send.at[3, k], q_recv.at[3, k], partner)
@@ -215,16 +227,18 @@
         at, pass_on = from_y(k)
         landed(at, n_recv.at[0, k])
         if k % 2 == 0:
-            onward(k).start()
+            onward_do(k, lambda copy: copy.start())
         pass_on.start()
         at, pass_on = from_z(k)
         landed(at, n_recv.at[1, k])
         if k % 2 == 1:
-            onward(k).start()
+            onward_do(k, lambda copy: copy.start())
         pass_on.start()
     for k in ORDER:
         at, pass_on = from_diag(k)
         landed(at, n_recv.at[2, k])
+        if k in ACROSS:
+            pl.when(c == x)(lambda: across(k).start())
         pass_on.start()
 
     for copy in tails:
@@ -236,7 +250,9 @@
         to_z.wait_send()
         to_p.wait_send()
         to_self.wait()
-        onward(k).wait_send()
+        onward_do(k, lambda copy: copy.wait_send())
+        if k in ACROSS:
+            pl.when(c == x)(lambda: across(k).wait_send())
         from_y(k)[1].wait_send()
         from_z(k)[1].wait_send()
         from_diag(k)[1].wait_send()
@@ -393,7 +409,7 @@
                 pltpu.VMEM((exp_local, d_model, f_loc), dtype), pltpu.VMEM((exp_local, f_loc, d_model), dtype),
                 buf13, buf2, buf13, buf2, buf13, buf2, buf13, buf2, dma((4,)),
                 dma((3, 8)), dma((3, 2, 4)), dma((3,)), dma((6,)), dma((6,)), dma((6,)), dma((6,)),
-                dma((3, 6)), dma((3, 6)), dma((4, 6)), dma((4, 6)), dma((6,)),
+                dma((3, 6)), dma((3, 6)), dma((6,)), dma((4, 6)), dma((4, 6)), dma((6,)),
             ],
             compiler_params=pltpu.CompilerParams(has_side_effects=True, vmem_limit_bytes=67043328),
         )(owner, offset, w_gate, w_up, w_down)

time: 831 us -> 821 us (0.988)
  Pallas kernels: 815 us -> 805 us
    pallas_call x1, Pallas kernels: 742 us -> 732 us  [device_body(): pl.pallas_call(move_kernel, out_shape=[shape(layers, home, d_model, 2 * f...]
where the time goes in v8:
time: 821 us; the launch traced here: 820 us
  Pallas kernels  805 us (98%)
  starting transfers between devices  10 us (1%)
    pallas_call x1, Pallas kernels, device_body(): pl.pallas_call(move_kernel, out_shape=[shape(layers, home, d_model, 2 * f...  732 us
    pallas_call x1, Pallas kernels, device_body(): pl.pallas_call(settle_kernel, out_shape=[shape(*o13.shape), shape(layers,...  69.6 us
  transfers between devices with their start and end apart: 4, of which 0 were waited for; matrix products, arithmetic and copies ran while one was open for 0% of the time, Pallas kernels for 8%

profile of v8, /device:TPU:2, one launch (start us, length us, event | category | flops | bytes accessed | tf_op | source)
XLA Modules:
  0.0 820.2 jit_solution(5904345502923780908)
XLA Ops:
  0.6 1.2 subtract_clamp_fusion
  1.8 731.9 %shard_map.75 = (bf16[2,2,2048,1536]{3,2,1,0:T(8,128)(2,1)}, bf16[2,768,2048]{2,1,0:T(8,128)(2,1)}, bf16[2,256,2048]{2,1,0:T(8,128)(2,1)}, bf16[2,4,2048,1536]{3...) custom-call(s32[4]{0:T(128)} %get-tuple-element.31.owner_ref, ...), custom_call_target="tpu_custom_call" | custom-call | tf_op jit(solution)/shard_map/pallas_call | solution.py:397
  733.7 1.9 collective-permute-start
  735.6 4.5 collective-permute-start.1
  740.2 0.1 collective-permute-start.2
  740.2 3.5 collective-permute-start.3
  743.8 0.0 copy-start
  743.8 1.6 copy-done
  745.4 69.6 %shard_map.76 = (bf16[2,2,2048,1536]{3,2,1,0:T(8,128)(2,1)}, bf16[2,2,768,2048]{3,2,1,0:T(8,128)(2,1)}, bf16[2,4,2048,1536]{3,2,1,0:T(8,128)(2,1)}, bf16[2,4,768,2048]{3,2,1,0:T(8,128)(2,1)}) custom-call(bf16[2,2,2048,1536]{3,2,1,0:T(8,128)(2,1)} %get-tuple-element.17.o13, bf16[2,768,2048]{2,1,0:T(8,128)(2,1)} %get-tuple-element.18.o2, ...), custom_call_target="tpu_custom_call" | custom-call | flops 1000000000 | bytes 213909504 | tf_op jit(solution)/shard_map/pallas_call | solution.py:418
  815.0 0.0 collective-permute-done.r0
  815.0 0.0 copy-start.1
  815.0 0.0 collective-permute-done.1.r1
  815.0 0.0 copy-start.2
  815.0 0.0 collective-permute-done.2.r2
  815.0 0.0 copy-start.3
  815.0 0.0 collective-permute-done.3.r3
  815.1 0.0 copy-start.4
  815.1 0.9 copy-done.1
  816.0 0.4 copy-done.2
  816.3 0.3 copy-done.3
  816.6 0.3 copy-done.4
  816.9 3.3 shard_map.77
Async XLA Ops:
  733.7 81.3 %collective-permute-start = (bf16[256,2048]{1,0:T(8,128)(2,1)}, bf16[256,2048]{1,0:T(8,128)(2,1)S(1)}, u32[]{:S(2)}, u32[]{:S(2)}) collective-permute-start(bf16[256,2048]{1,0:T(8,128)(2,1)} %get-tuple-element.23.t0), channel_id=1, source_target_pairs={{1,3},{2,4},{3,7},{4,1},{5,2},{6,5},{7,6},{9,11},{10,12},{11,15},{... | collective-permute-start | bytes 3145736 | tf_op jit(solution)/shard_map/ppermute | solution.py:416
  735.6 79.4 %collective-permute-start.1 = (bf16[256,2048]{1,0:T(8,128)(2,1)}, bf16[256,2048]{1,0:T(8,128)(2,1)S(1)}, u32[]{:S(2)}, u32[]{:S(2)}) collective-permute-start(bf16[256,2048]{1,0:T(8,128)(2,1)} %get-tuple-element.24.t1), channel_id=1, source_target_pairs={{0,1},{1,2},{2,5},{3,6},{4,0},{5,3},{6,4},{8,9},{9,10},{10,13},{11... | collective-permute-start | bytes 3145736 | tf_op jit(solution)/shard_map/ppermute | solution.py:416
  740.2 74.9 %collective-permute-start.2 = (bf16[256,2048]{1,0:T(8,128)(2,1)}, bf16[256,2048]{1,0:T(8,128)(2,1)S(1)}, u32[]{:S(2)}, u32[]{:S(2)}) collective-permute-start(bf16[256,2048]{1,0:T(8,128)(2,1)} %get-tuple-element.25), channel_id=1, source_target_pairs={{0,8},{1,11},{2,12},{3,15},{4,9},{5,10},{6,13},{7,14},{8,0},{9,3},... | collective-permute-start | bytes 3145736 | tf_op jit(solution)/shard_map/ppermute | solution.py:416
  740.2 74.8 %collective-permute-start.3 = (bf16[256,2048]{1,0:T(8,128)(2,1)}, bf16[256,2048]{1,0:T(8,128)(2,1)S(1)}, u32[]{:S(2)}, u32[]{:S(2)}) collective-permute-start(bf16[256,2048]{1,0:T(8,128)(2,1)} %get-tuple-element.26), channel_id=1, source_target_pairs={{0,9},{1,10},{2,13},{3,14},{4,8},{5,11},{6,12},{7,15},{8,1},{9,2},... | collective-permute-start | bytes 3145736 | tf_op jit(solution)/shard_map/ppermute | solution.py:416
  743.8 1.6 copy-start
  815.0 1.0 copy-start.1
  815.0 1.3 copy-start.2
  815.0 1.6 copy-start.3
  815.1 1.9 copy-start.4
